TPU v7x, 1024 devices: a whole 4x8x16 slice. The times are simulated.
1024 devices in a mesh: section: 128 (over z_hi, y, x, core), tensor: 8 (over z_lo).
Axes of the slice: x: 4, y: 8, z: 16 (z_hi: 2, z_lo: 8; z = z_hi * 8 + z_lo), core: 2. Of those that a mesh axis runs over, the one named last changes fastest.
Arguments:
- acts: bfloat16 [128, 2, 32, 4096], P('section', None, None, 'tensor'), may hold values from -6 to 6
- grads_in: bfloat16 [128, 2, 32, 4096], P('section', None, None, 'tensor'), may hold values from -6 to 6
- head_grads: bfloat16 [128, 2, 128, 1024], P('section', None, None, 'tensor'), may hold values from -6 to 6
- types: int32 [128, 2, 32], P('section'), may hold values 0 or 1
- gains: bfloat16 [128, 2, 2, 1024], P('section'), may hold values from 0.3984375 to 1.59375
- w_query: bfloat16 [128, 2, 4096, 1024], P('section', None, None, 'tensor'), may hold values from -0.09375 to 0.09375
- w_key: bfloat16 [128, 2, 4096, 128], P('section', None, None, 'tensor'), may hold values from -0.09375 to 0.09375
- w_value: bfloat16 [128, 2, 4096, 128], P('section', None, None, 'tensor'), may hold values from -0.09375 to 0.09375
Outputs:
- routed: bfloat16 [128, 2, 32, 4096], P('section', None, None, 'tensor')
All inputs are finite; a program needn't handle non-finite values. No bound on the sum of `types` on one device may be relied on, other than what follows from the above.
Results may differ from a plain program's by a relative error of at most 0.0055.
Values may be sent and summed in bfloat16 or wider, within the bound.
No kernel may reach another device: no remote copies, remote signals or barrier semaphores. Data moves between devices by JAX's collectives and lax.ppermute only.
A program may use at most 64 MiB of HBM per device.

v0:
```python
import jax
import jax.numpy as jnp
from jax import lax
from jax.sharding import PartitionSpec as P

HEAD_DIM = 128
SUB = 4


epsilon = 1e-05


def swapped(value, axis, stride):
    mask = 2**stride
    pairs = [(source, source ^ mask) for source in range(lax.axis_size(axis))]
    return lax.ppermute(value, axis, pairs)


def from_everyone(value, axis):
    peers = lax.axis_size(axis)
    return lax.all_to_all(
        jnp.broadcast_to(value[None], (peers, *value.shape)), axis, 0, 0, tiled=True
    )


def in_order(parts, dim):
    shape = list(parts.shape[1:])
    shape[dim] *= parts.shape[0]
    return jnp.moveaxis(parts, 0, dim).reshape(shape)


def gathered_copies(value, axis, dim):
    parts = from_everyone(value, axis)
    return in_order(parts, dim)


def turned_gather(arrays, axis, dims):
    turned = [jnp.moveaxis(a, dim, 0) for a, dim in zip(arrays, dims)]
    both = jnp.concatenate([t.reshape(len(t), -1) for t in turned], axis=1)
    whole, at, done = (lax.all_gather(both, axis, axis=0, tiled=True), 0, [])
    for t, dim in zip(turned, dims):
        piece = whole[:, at : at + t[0].size].reshape(-1, *t.shape[1:])
        done.append(jnp.moveaxis(piece, 0, dim))
        at += t[0].size
    return tuple(done)


def shifted(value, axis, by):
    peers = lax.axis_size(axis)
    return lax.ppermute(value, axis, [(i, (i + by) % peers) for i in range(peers)])


def sum_columns(first, second):
    return (
        lax.psum_scatter(first, "tensor", scatter_dimension=2, tiled=True),
        lax.psum_scatter(second, "tensor", scatter_dimension=2, tiled=True),
    )


def collect_rows(member, position, levels, axis):
    for bit in range(levels):
        partner = swapped(member, "section", bit)
        upper_bit = position >> bit & 1
        member = jnp.where(
            upper_bit == 1,
            jnp.concatenate([partner, member], axis=axis),
            jnp.concatenate([member, partner], axis=axis),
        )
    return member


def halve_once(member, upper_bit, bit):
    half_rows = member.shape[1] // 2
    lower_rows = member[:, :half_rows]
    higher_rows = member[:, half_rows:]
    kept_rows = jnp.where(upper_bit == 1, higher_rows, lower_rows)
    sent_rows = jnp.where(upper_bit == 1, lower_rows, higher_rows)
    return kept_rows + swapped(sent_rows, "section", bit)


def reduce_rows(first, second, position, levels):
    for bit in reversed(range(levels)):
        upper_bit = position >> bit & 1
        first = halve_once(first, upper_bit, bit)
        second = halve_once(second, upper_bit, bit)
    return (first, second)


def per_device(acts, grads_in, head_grads, types, gains, w_query, w_key, w_value):
    tensors = lax.axis_size("tensor")
    section_count = lax.axis_size("section") // SUB
    levels = SUB.bit_length() - 1
    position = lax.axis_index("section") % SUB
    section_here = lax.axis_index("section") // SUB
    x_local = acts[0]
    grad_local = grads_in[0]
    out_grads = head_grads[0]
    w_query = w_query[0]
    w_key = w_key[0]
    w_value = w_value[0]
    x_cols = gathered_copies(x_local, "tensor", 2)
    x_full = collect_rows(x_cols, position, levels, 1)
    kind_full = collect_rows(types[0].astype(jnp.bfloat16), position, levels, 1)
    gain_full = collect_rows(gains[0], position, levels, 2).astype(jnp.float32)
    tokens = x_full.shape[1]
    tokq = x_local.shape[1]
    width = x_full.shape[2]
    cols_dev = x_local.shape[2]
    x_float = x_full.astype(jnp.float32)
    inverse = lax.rsqrt(jnp.mean(x_float * x_float, axis=-1, keepdims=True) + epsilon)
    gain_rows = jnp.where(kind_full[..., None] > 0.5, gain_full[:, 1:2, :], gain_full[:, 0:1, :])
    normed = (x_float * inverse * gain_rows).astype(jnp.bfloat16)
    queries = jnp.einsum(
        "ctd,cdh->cth", normed, w_query, preferred_element_type=jnp.float32
    ).astype(jnp.bfloat16)
    key_part = jnp.einsum("ctd,cdh->cth", normed, w_key, preferred_element_type=jnp.float32).astype(
        jnp.bfloat16
    )
    value_part = jnp.einsum(
        "ctd,cdh->cth", normed, w_value, preferred_element_type=jnp.float32
    ).astype(jnp.bfloat16)
    key_rows, value_rows = turned_gather((key_part, value_part), "tensor", (2, 2))
    softmax_scale = HEAD_DIM ** (-0.5)
    scores = (
        jnp.einsum("cqh,ckh->cqk", queries, key_rows, preferred_element_type=jnp.float32)
        * softmax_scale
    )
    causal = jnp.arange(tokens)[:, None] >= jnp.arange(tokens)[None, :]
    scores = jnp.where(causal[None], scores, -1e30)
    attn_probs = jax.nn.softmax(scores, axis=-1)
    probs_low = attn_probs.astype(jnp.bfloat16)
    prob_grads = jnp.einsum(
        "cqh,ckh->cqk", out_grads, value_rows, preferred_element_type=jnp.float32
    )
    score_grads = (
        attn_probs
        * (prob_grads - jnp.sum(prob_grads * attn_probs, axis=-1, keepdims=True))
        * softmax_scale
    ).astype(jnp.bfloat16)
    query_grads = jnp.einsum(
        "cqk,ckh->cqh", score_grads, key_rows, preferred_element_type=jnp.float32
    ).astype(jnp.bfloat16)
    key_each = jnp.einsum("cqk,cqh->ckh", score_grads, queries, preferred_element_type=jnp.float32)
    value_each = jnp.einsum(
        "cqk,cqh->ckh", probs_low, out_grads, preferred_element_type=jnp.float32
    )
    key_sum, value_sum = sum_columns(key_each, value_each)
    key_grads = key_sum.astype(jnp.bfloat16)
    value_grads = value_sum.astype(jnp.bfloat16)
    joined_grads = jnp.concatenate([query_grads, key_grads, value_grads], axis=2)
    joined_weights = jnp.concatenate([w_query, w_key, w_value], axis=2)
    partial_value = jnp.einsum(
        "cth,cdh->ctd", joined_grads, joined_weights, preferred_element_type=jnp.float32
    )
    stat_part = jnp.sum(x_float * gain_rows * partial_value, axis=-1)
    stat_wide = jnp.broadcast_to(stat_part[..., None], stat_part.shape + (tensors,))
    grad_cols_sum, stat_cols = sum_columns(partial_value, stat_wide)
    grad_mine, stat_mine = reduce_rows(grad_cols_sum, stat_cols, position, levels)
    my_inverse = lax.dynamic_slice_in_dim(inverse, position * tokq, tokq, 1)
    my_gain = lax.dynamic_slice_in_dim(gain_rows, position * tokq, tokq, 1)
    my_gain = lax.dynamic_slice_in_dim(my_gain, lax.axis_index("tensor") * cols_dev, cols_dev, 2)
    my_x = x_local.astype(jnp.float32)
    stat_mean = stat_mine / width
    norm_grads = my_inverse * my_gain * grad_mine - my_x * my_inverse**3 * stat_mean
    result = (grad_local.astype(jnp.float32) + norm_grads).astype(jnp.bfloat16)
    arrived = shifted(result, "section", -SUB)
    routed = jnp.where(section_here == section_count - 1, arrived[::-1], arrived)
    return routed[None]


def solution(mesh):
    return jax.shard_map(
        per_device,
        mesh=mesh,
        in_specs=(
            P("section", None, None, "tensor"),
            P("section", None, None, "tensor"),
            P("section", None, None, "tensor"),
            P("section", None, None),
            P("section", None, None, None),
            P("section", None, None, "tensor"),
            P("section", None, None, "tensor"),
            P("section", None, None, "tensor"),
        ),
        out_specs=P("section", None, None, "tensor"),
        check_vma=False,
    )
```

profile of v0, /device:TPU:61, one launch (start us, length us, event | category | flops | bytes accessed | tf_op | source)
XLA Modules:
  0.0 424.4 jit_solution(9780260936084059242)
XLA Ops:
  6.5 1.7 broadcast_in_dim.65
  8.3 15.4 %all-to-all-start = ((bf16[8,2,32,512]{3,2,1,0:T(8,128)(2,1)}), bf16[8,2,32,512]{3,2,1,0:T(8,128)(2,1)S(1)}, u32[]{:S(2)}, u32[]{:S(2)}) async-start(bf16[8,2,32,512]{3,2,1,0:T(8,128)(2,1)} %broadcast_in_dim.65), calls=%async_computation | async-start | bytes 1048576 | tf_op jit(solution)/shard_map/all_to_all | solution.py:21
  23.7 0.0 reduce-scatter.6.cloned.1.call-start
  23.7 0.7 convert_bitcast_fusion
  24.4 2.9 collective-permute-start.2
  27.3 1.9 collective-permute-start.4
  29.3 0.1 broadcast_select_fusion.5
  29.4 2.8 collective-permute-start.3
  32.2 0.8 broadcast_select_fusion.2
  33.0 2.5 collective-permute-start.5
  35.5 9.2 %all-to-all-done = bf16[8,2,32,512]{3,2,1,0:T(8,128)(2,1)S(1)} async-done(((bf16[8,2,32,512]{3,2,1,0:T(8,128)(2,1)}), bf16[8,2,32,512]{3,2,1,0:T(8,128)(2,1)S(1)}, u32[]{:S(2)}, u32[]{:S(2)}) %all-to-all-start) | async-done | bytes 524320 | tf_op jit(solution)/shard_map/all_to_all | solution.py:21
  44.7 10.6 %collective-permute-start = (bf16[2,32,4096]{2,1,0:T(8,128)(2,1)S(1)}, bf16[2,32,4096]{2,1,0:T(8,128)(2,1)S(1)}, u32[]{:S(2)}, u32[]{:S(2)}) collective-permute-start(bf16[2,32,4096]{2,1,0:T(8,128)(2,1)S(1)} %bitcast.68), channel_id=1, source_target_pairs={{0,8},{8,0},{16,24},{24,16},{32,40},{40,32},{48,56},{56,48},{64,72... | collective-permute-start | bytes 1572872 | tf_op jit(solution)/shard_map/ppermute | solution.py:16
  55.4 0.1 fusion.50
  55.5 1.4 collective-permute-done
  56.9 0.2 maximum_select_fusion.1
  57.1 2.8 collective-permute-start.1
  59.9 0.1 fusion.59
  60.0 0.1 copy_bitcast_fusion
  60.1 23.3 %collective-permute-done.1 = bf16[2,64,4096]{2,1,0:T(8,128)(2,1)S(1)} collective-permute-done((bf16[2,64,4096]{2,1,0:T(8,128)(2,1)S(1)}, bf16[2,64,4096]{2,1,0:T(8,128)(2,1)S(1)}, u32[]{:S(2)}, u32[]{:S(2)}) %collective-permute-start.1) | collective-permute-done | bytes 1048608 | tf_op jit(solution)/shard_map/ppermute | solution.py:16
  83.3 0.8 fusion.2
  84.1 1.2 fusion.25
  85.4 1.2 fusion.26
  86.6 39.9 %all_gather.3 = bf16[128,512]{1,0:T(8,128)(2,1)S(1)} all-gather(bf16[16,512]{1,0:T(8,128)(2,1)S(1)} %pad_maximum_fusion), channel_id=1, replica_groups=mesh['section'=128,'tensor'=8] {'tensor'}, dimensions={0}, use_global_device_ids=true | all-gather | bytes 147456 | tf_op jit(solution)/shard_map/all_gather | solution.py:40
  126.5 0.1 copy.23
  126.7 0.1 copy.22
  126.8 2.7 fusion.22
  129.6 0.2 fusion.18
  129.7 0.7 fusion.60
  130.4 0.9 fusion.42
  131.3 0.0 reduce-scatter.6.cloned.1.call-update
  131.3 0.0 reduce-scatter.4.cloned.1.call-start
  131.4 0.2 convolution_bitcast_fusion
  131.6 1.8 fusion.27
  133.4 0.0 reduce-scatter.4.cloned.1.call-update
  133.4 0.0 reduce-scatter.8.cloned.1.call-start
  133.5 2.8 copy.18
  136.3 1.2 convolution_convert_fusion
  137.5 62.1 %reduce-scatter.6.cloned.1.call-done = f32[2,128,16]{1,2,0:T(8,128)} async-done(((f32[2,128,128]{1,2,0:T(8,128)}), f32[2,128,16]{1,2,0:T(8,128)}) %reduce-scatter.6.cloned.1.call-update) | async-done | bytes 16400 | tf_op jit(solution)/shard_map/reduce_scatter | solution.py:56
  199.6 0.7 convert_element_type.75
  200.3 64.0 %reduce-scatter.4.cloned.1.call-done = f32[2,128,16]{1,2,0:T(8,128)} async-done(((f32[2,128,128]{1,2,0:T(8,128)}), f32[2,128,16]{1,2,0:T(8,128)}) %reduce-scatter.4.cloned.1.call-update) | async-done | bytes 16400 | tf_op jit(solution)/shard_map/reduce_scatter | solution.py:55
  264.4 0.7 convert_element_type.73
  265.1 6.2 %fusion.6 = (f32[2,128]{1,0:T(2,128)S(1)}, f32[2,128,4096]{2,1,0:T(8,128)}, f32[2,128,4096]{2,1,0:T(8,128)}) fusion(f32[2,4096]{1,0:T(2,128)S(1)} %copy-done.6, f32[2,4096]{1,0:T(2,128)S(1)} %copy-done.8, pred[2,128]{1,0:T(4,128)(4,1)} %copy-done.11, bf16[2,64,4096]{2,1,0:T(8,128)(2,1)} %copy-done.2, bf16[2,64,4096]{2,1,0:T(8,128)(2,1)S(1)} %maximum_select_fusion.1, ...), kind=kOutput, calls=%fused_computation.9 | convolution fusion | flops 358334208 | bytes 13255937 | tf_op jit(solution)/shard_map/cth,cdh->ctd/dot_general | solution.py:152
  271.3 0.0 reduce-scatter.8.cloned.1.call-update
  271.3 1.3 dynamic-slice.4
  272.6 0.1 fusion.49
  272.7 22.4 %all-reduce = f32[2,128,8]{1,0,2:T(2,128)S(1)} all-reduce(f32[2,128,8]{1,0,2:T(2,128)S(1)} %broadcast_in_dim.73), channel_id=5, replica_groups=mesh['section'=128,'tensor'=8] {'tensor'}, use_global_device_ids=true, to_apply=%region_8.9.clone | all-reduce | flops 2048 | bytes 16384
  295.1 0.7 constant_dynamic-slice_fusion
  295.8 0.1 broadcast_select_fusion.3
  295.8 2.8 collective-permute-start.8
  298.6 80.3 %reduce-scatter.8.cloned.1.call-done = f32[2,128,512]{2,1,0:T(8,128)} async-done(((f32[2,128,4096]{2,1,0:T(8,128)}), f32[2,128,512]{2,1,0:T(8,128)}) %reduce-scatter.8.cloned.1.call-update) | async-done | bytes 524304 | tf_op jit(solution)/shard_map/reduce_scatter | solution.py:55
  378.9 1.1 slice_select_fusion
  380.0 2.8 collective-permute-start.6
  382.8 0.1 select_add_fusion.1
  382.9 0.1 broadcast_select_fusion.4
  382.9 3.3 collective-permute-start.9
  386.2 2.4 collective-permute-done.6
  388.6 1.1 select_add_fusion
  389.8 3.8 collective-permute-start.7
  393.6 0.1 multiply_bitcast_fusion
  393.7 0.9 collective-permute-done.7
  394.6 1.1 fusion.35
  395.7 2.2 collective-permute-start.10
  397.9 19.3 %collective-permute-done.10 = bf16[2,32,512]{2,1,0:T(8,128)(2,1)S(1)} collective-permute-done((bf16[2,32,512]{2,1,0:T(8,128)(2,1)S(1)}, bf16[2,32,512]{2,1,0:T(8,128)(2,1)S(1)}, u32[]{:S(2)}, u32[]{:S(2)}) %collective-permute-start.10) | collective-permute-done | bytes 65568 | tf_op jit(solution)/shard_map/ppermute | solution.py:50
  417.2 0.6 fusion.41
  (44 shorter events, 0.2 us)
Async XLA Ops:
  6.5 123.9 %copy-start = (bf16[1,2,128,128]{3,2,1,0:T(8,128)(2,1)S(1)}, bf16[1,2,128,128]{3,2,1,0:T(8,128)(2,1)}, u32[]{:S(2)}) copy-start(bf16[1,2,128,128]{3,2,1,0:T(8,128)(2,1)} %param.10) | copy-start | bytes 196612
  6.5 77.6 %copy-start.13 = (bf16[1,2,4096,16]{2,3,1,0:T(8,128)(2,1)S(1)}, bf16[1,2,4096,16]{2,3,1,0:T(8,128)(2,1)}, u32[]{:S(2)}) copy-start(bf16[1,2,4096,16]{2,3,1,0:T(8,128)(2,1)} %param.14) | copy-start | bytes 786436
  8.3 36.4 %all-to-all-start = ((bf16[8,2,32,512]{3,2,1,0:T(8,128)(2,1)}), bf16[8,2,32,512]{3,2,1,0:T(8,128)(2,1)S(1)}, u32[]{:S(2)}, u32[]{:S(2)}) async-start(bf16[8,2,32,512]{3,2,1,0:T(8,128)(2,1)} %broadcast_in_dim.65), calls=%async_computation | async-start | bytes 1048576 | tf_op jit(solution)/shard_map/all_to_all | solution.py:21
  23.7 175.9 %reduce-scatter.6.cloned.1.call-start = ((), (), s32[]{:S(2)}) async-start(), calls=%async_computation.5 | async-start | bytes 147456 | tf_op jit(solution)/shard_map/reduce_scatter | solution.py:56
  24.4 4.8 %collective-permute-start.2 = (bf16[2,32]{1,0:T(2,128)(2,1)S(1)}, bf16[2,32]{1,0:T(2,128)(2,1)S(1)}, u32[]{:S(2)}, u32[]{:S(2)}) collective-permute-start(bf16[2,32]{1,0:T(2,128)(2,1)S(1)} %convert_bitcast_fusion), channel_id=1, source_target_pairs={{0,8},{8,0},{16,24},{24,16},{32,40},{40,32},{48,56},{56,48},{64,72... | collective-permute-start | bytes 392 | tf_op jit(solution)/shard_map/ppermute | solution.py:16
  27.3 4.9 %collective-permute-start.4 = (bf16[2,2,1024]{2,1,0:T(2,128)(2,1)}, bf16[2,2,1024]{2,1,0:T(2,128)(2,1)S(1)}, u32[]{:S(2)}, u32[]{:S(2)}) collective-permute-start(bf16[2,2,1024]{2,1,0:T(2,128)(2,1)} %bitcast.78), channel_id=1, source_target_pairs={{0,8},{8,0},{16,24},{24,16},{32,40},{40,32},{48,56},{56,48},{64,72... | collective-permute-start | bytes 24584 | tf_op jit(solution)/shard_map/ppermute | solution.py:16
  29.4 26.0 %collective-permute-start.3 = (bf16[2,64]{1,0:T(2,128)(2,1)S(1)}, bf16[2,64]{1,0:T(2,128)(2,1)S(1)}, u32[]{:S(2)}, u32[]{:S(2)}) collective-permute-start(bf16[2,64]{1,0:T(2,128)(2,1)S(1)} %broadcast_select_fusion.5), channel_id=1, source_target_pairs={{0,16},{8,24},{16,0},{24,8},{32,48},{40,56},{48,32},{56,40},{64,80... | collective-permute-start | bytes 776 | tf_op jit(solution)/shard_map/ppermute | solution.py:16
  33.0 22.5 %collective-permute-start.5 = (bf16[2,2,2048]{2,1,0:T(2,128)(2,1)S(1)}, bf16[2,2,2048]{2,1,0:T(2,128)(2,1)S(1)}, u32[]{:S(2)}, u32[]{:S(2)}) collective-permute-start(bf16[2,2,2048]{2,1,0:T(2,128)(2,1)S(1)} %broadcast_select_fusion.2), channel_id=1, source_target_pairs={{0,16},{8,24},{16,0},{24,8},{32,48},{40,56},{48,32},{56,40},{64,80... | collective-permute-start | bytes 49160 | tf_op jit(solution)/shard_map/ppermute | solution.py:16
  44.7 12.2 %collective-permute-start = (bf16[2,32,4096]{2,1,0:T(8,128)(2,1)S(1)}, bf16[2,32,4096]{2,1,0:T(8,128)(2,1)S(1)}, u32[]{:S(2)}, u32[]{:S(2)}) collective-permute-start(bf16[2,32,4096]{2,1,0:T(8,128)(2,1)S(1)} %bitcast.68), channel_id=1, source_target_pairs={{0,8},{8,0},{16,24},{24,16},{32,40},{40,32},{48,56},{56,48},{64,72... | collective-permute-start | bytes 1572872 | tf_op jit(solution)/shard_map/ppermute | solution.py:16
  55.4 29.9 %copy-start.11 = (pred[2,128]{1,0:T(4,128)(4,1)}, pred[2,128]{1,0:T(4,128)(4,1)S(1)}, u32[]{:S(2)}) copy-start(pred[2,128]{1,0:T(4,128)(4,1)S(1)} %fusion.50) | copy-start | bytes 772
  57.1 26.2 %collective-permute-start.1 = (bf16[2,64,4096]{2,1,0:T(8,128)(2,1)S(1)}, bf16[2,64,4096]{2,1,0:T(8,128)(2,1)S(1)}, u32[]{:S(2)}, u32[]{:S(2)}) collective-permute-start(bf16[2,64,4096]{2,1,0:T(8,128)(2,1)S(1)} %maximum_select_fusion.1), channel_id=1, source_target_pairs={{0,16},{8,24},{16,0},{24,8},{32,48},{40,56},{48,32},{56,40},{64,80... | collective-permute-start | bytes 3145736 | tf_op jit(solution)/shard_map/ppermute | solution.py:16
  60.0 66.7 %copy-start.5 = (f32[2,4096]{1,0:T(2,128)}, f32[2,4096]{1,0:T(2,128)S(1)}, u32[]{:S(2)}) copy-start(f32[2,4096]{1,0:T(2,128)S(1)} %get-tuple-element.16) | copy-start | bytes 98308
  60.0 66.7 %copy-start.7 = (f32[2,4096]{1,0:T(2,128)}, f32[2,4096]{1,0:T(2,128)S(1)}, u32[]{:S(2)}) copy-start(f32[2,4096]{1,0:T(2,128)S(1)} %get-tuple-element.17) | copy-start | bytes 98308
  83.3 2.0 copy-start.2
  84.1 1.3 copy-start.9
  84.1 1.2 copy-start.12
  85.4 41.4 %copy-start.1 = (bf16[1,2,4096,128]{3,2,1,0:T(8,128)(2,1)S(1)}, bf16[1,2,4096,128]{3,2,1,0:T(8,128)(2,1)}, u32[]{:S(2)}) copy-start(bf16[1,2,4096,128]{3,2,1,0:T(8,128)(2,1)} %param.13) | copy-start | bytes 6291460
  131.3 133.0 %reduce-scatter.4.cloned.1.call-start = ((), (), s32[]{:S(2)}) async-start(), calls=%async_computation.4 | async-start | bytes 147456 | tf_op jit(solution)/shard_map/reduce_scatter | solution.py:55
  131.6 133.5 %copy-start.6 = (f32[2,4096]{1,0:T(2,128)S(1)}, f32[2,4096]{1,0:T(2,128)}, u32[]{:S(2)}) copy-start(f32[2,4096]{1,0:T(2,128)} %copy-done.5) | copy-start | bytes 98308
  131.6 133.5 %copy-start.8 = (f32[2,4096]{1,0:T(2,128)S(1)}, f32[2,4096]{1,0:T(2,128)}, u32[]{:S(2)}) copy-start(f32[2,4096]{1,0:T(2,128)} %copy-done.7) | copy-start | bytes 98308
  133.4 245.5 %reduce-scatter.8.cloned.1.call-start = ((), (), s32[]{:S(2)}) async-start(), calls=%async_computation.6 | async-start | bytes 4718592 | tf_op jit(solution)/shard_map/reduce_scatter | solution.py:55
  271.3 1.4 copy-start.10
  271.3 123.3 %copy-start.3 = (bf16[1,2,32,512]{3,2,1,0:T(8,128)(2,1)S(1)}, bf16[1,2,32,512]{3,2,1,0:T(8,128)(2,1)}, u32[]{:S(2)}) copy-start(bf16[1,2,32,512]{3,2,1,0:T(8,128)(2,1)} %param.8) | copy-start | bytes 196612
  271.3 123.3 %copy-start.4 = (bf16[1,2,32,512]{3,2,1,0:T(8,128)(2,1)S(1)}, bf16[1,2,32,512]{3,2,1,0:T(8,128)(2,1)}, u32[]{:S(2)}) copy-start(bf16[1,2,32,512]{3,2,1,0:T(8,128)(2,1)} %param.9) | copy-start | bytes 196612
  295.8 86.9 %collective-permute-start.8 = (f32[2,64,1]{1,0,2:T(2,128)S(1)}, f32[2,64,1]{1,0,2:T(2,128)S(1)}, u32[]{:S(2)}, u32[]{:S(2)}) collective-permute-start(f32[2,64,1]{1,0,2:T(2,128)S(1)} %broadcast_select_fusion.3), channel_id=1, source_target_pairs={{0,16},{8,24},{16,0},{24,8},{32,48},{40,56},{48,32},{56,40},{64,80... | collective-permute-start | bytes 1544 | tf_op jit(solution)/shard_map/ppermute | solution.py:16
  380.0 8.7 %collective-permute-start.6 = (f32[2,64,512]{2,1,0:T(8,128)S(1)}, f32[2,64,512]{2,1,0:T(8,128)S(1)}, u32[]{:S(2)}, u32[]{:S(2)}) collective-permute-start(f32[2,64,512]{2,1,0:T(8,128)S(1)} %slice_select_fusion), channel_id=1, source_target_pairs={{0,16},{8,24},{16,0},{24,8},{32,48},{40,56},{48,32},{56,40},{64,80... | collective-permute-start | bytes 786440 | tf_op jit(solution)/shard_map/ppermute | solution.py:16
  382.9 10.7 %collective-permute-start.9 = (f32[2,32,1]{1,0,2:T(2,128)S(1)}, f32[2,32,1]{1,0,2:T(2,128)S(1)}, u32[]{:S(2)}, u32[]{:S(2)}) collective-permute-start(f32[2,32,1]{1,0,2:T(2,128)S(1)} %broadcast_select_fusion.4), channel_id=1, source_target_pairs={{0,8},{8,0},{16,24},{24,16},{32,40},{40,32},{48,56},{56,48},{64,72... | collective-permute-start | bytes 776 | tf_op jit(solution)/shard_map/ppermute | solution.py:16
  389.8 4.8 %collective-permute-start.7 = (f32[2,32,512]{2,1,0:T(8,128)S(1)}, f32[2,32,512]{2,1,0:T(8,128)S(1)}, u32[]{:S(2)}, u32[]{:S(2)}) collective-permute-start(f32[2,32,512]{2,1,0:T(8,128)S(1)} %slice_select_fusion.1), channel_id=1, source_target_pairs={{0,8},{8,0},{16,24},{24,16},{32,40},{40,32},{48,56},{56,48},{64,72... | collective-permute-start | bytes 393224 | tf_op jit(solution)/shard_map/ppermute | solution.py:16
  395.7 21.5 %collective-permute-start.10 = (bf16[2,32,512]{2,1,0:T(8,128)(2,1)S(1)}, bf16[2,32,512]{2,1,0:T(8,128)(2,1)S(1)}, u32[]{:S(2)}, u32[]{:S(2)}) collective-permute-start(bf16[2,32,512]{2,1,0:T(8,128)(2,1)S(1)} %fusion.35), channel_id=1, source_target_pairs={{0,992},{8,1000},{16,1008},{24,1016},{32,0},{40,8},{48,16},{56,24}... | collective-permute-start | bytes 196616 | tf_op jit(solution)/shard_map/ppermute | solution.py:50
Sparse Core Ops, SparseCore 0:
  131.5 68.0 reduce-scatter.5
  203.0 61.3 reduce-scatter.3
  271.4 107.4 reduce-scatter.7
where the time goes:
time: 425 us; the launch traced here: 424 us
  waiting for transfers between devices  263 us (62%)
  blocking collectives  62.3 us (15%)
  starting transfers between devices  53.9 us (13%)
  matrix products  15.6 us (4%)
  between operations  13.6 us (3%)
  other arithmetic  9.09 us (2%)
  local copies, waits for them, and re-layouts  6.91 us (2%)
    reduce_scatter x2, waiting for transfers between devices, sum_columns(): lax.psum_scatter(first, 'tensor', scatter_dimension=2, tiled=True)  144 us
    reduce_scatter x1, waiting for transfers between devices, sum_columns(): lax.psum_scatter(second, 'tensor', scatter_dimension=2, tiled=True)  62.1 us
    all_gather x1, blocking collectives, turned_gather(): whole, at, done = (lax.all_gather(both, axis, axis=0, tiled=True), 0, [])  39.9 us
    ppermute x10, starting transfers between devices, swapped(): return lax.ppermute(value, axis, pairs)  36.2 us
    ppermute x10, waiting for transfers between devices, swapped(): return lax.ppermute(value, axis, pairs)  28 us
    unnamed x1, blocking collectives  22.4 us
    ppermute x1, waiting for transfers between devices, shifted(): lax.ppermute(value, axis, [(i, (i + by) % peers) for i in range(peers)])  19.3 us
    all_to_all x1, starting transfers between devices, from_everyone(): lax.all_to_all(jnp.broadcast_to(value[None], (peers, *value.shape)), axis...  15.4 us
  transfers between devices with their start and end apart: 15, of which 9 were waited for; matrix products, arithmetic and copies ran while one was open for 3% of the time, Pallas kernels for 0%

commit v1 on v0

v1 whole, which is shorter than its diff:
```python
import jax
import jax.numpy as jnp
from jax import lax
from jax.experimental import pallas as pl
from jax.experimental.pallas import tpu as pltpu
from jax.sharding import PartitionSpec as P


HEAD_DIM = 128
SUB = 4
ROW_MASKS = (0, 2, 1, 3)

epsilon = 1e-05
F32 = jnp.float32
BF16 = jnp.bfloat16


def swapped(value, axis, mask):
    pairs = [(source, source ^ mask) for source in range(lax.axis_size(axis))]
    return lax.ppermute(value, axis, pairs)


def shifted(value, by):
    peers = lax.axis_size("section")
    return lax.ppermute(value, "section", [(i, (i + by) % peers) for i in range(peers)])


def blocks_by(value, axis, count, here, masks):
    size = value.shape[axis] // count
    return jnp.concatenate(
        [lax.dynamic_slice_in_dim(value, (here ^ m) * size, size, axis) for m in masks], axis=axis
    )


def in_quads(parts):
    tensors = lax.axis_size("tensor")
    groups = [[first + i for i in range(4)] for first in range(0, tensors, 4)]
    return lax.all_to_all(parts, "tensor", 0, 0, axis_index_groups=groups, tiled=True)


def exchanged(parts):
    return lax.all_to_all(parts, "tensor", 0, 0, tiled=True)


def copies(value, count):
    return jnp.broadcast_to(value[None], (count, *value.shape))


def norm_kernel(column, *refs):
    parts, (kind, gain, w_kv, normed, kv, inverse) = refs[:SUB], refs[SUB:]
    quads, halves, _, rows, cols = parts[0].shape
    width = quads * halves * cols
    upper = column[0] // quads
    for j, part in enumerate(parts):
        total = jnp.zeros((rows, cols), F32)
        for i in range(quads):
            for h in range(halves):
                x = part[i, h, 0].astype(F32)
                total = total + x * x
        inv = lax.rsqrt(jnp.sum(total, axis=1, keepdims=True) / width + epsilon)
        at_rows = pl.ds(j * rows, rows)
        inverse[0, at_rows, :] = inv
        speech = kind[0, at_rows, :] > 0.5
        for i in range(quads):
            for h in range(halves):
                block = (upper ^ h) * quads + i
                at = pl.ds(pl.multiple_of(block * cols, cols), cols)
                rates = jnp.where(speech, gain[0, 1:2, at], gain[0, 0:1, at])
                normed[0, at_rows, at] = (part[i, h, 0].astype(F32) * inv * rates).astype(BF16)
    kv[0] = lax.dot_general(
        w_kv[0], normed[0], (((1,), (1,)), ((), ())), preferred_element_type=F32
    ).astype(BF16)


def normalised(column, parts, kind, gain, w_kv):
    quads, halves, spans, rows, cols = parts[0].shape
    tokens = SUB * rows
    width = quads * halves * cols
    channels = w_kv.shape[1]
    x_spec = pl.BlockSpec((quads, halves, 1, rows, cols), lambda n: (0, 0, n, 0, 0))

    def whole(*shape):
        return pl.BlockSpec((1, *shape), lambda n: (n, 0, 0))

    return pl.pallas_call(
        norm_kernel,
        grid=(spans,),
        in_specs=[pl.BlockSpec(memory_space=pltpu.SMEM)]
        + [x_spec] * SUB
        + [whole(tokens, 1), whole(2, width), whole(channels, width)],
        out_specs=[whole(tokens, width), whole(channels, tokens), whole(tokens, 1)],
        out_shape=[
            jax.ShapeDtypeStruct((spans, tokens, width), BF16),
            jax.ShapeDtypeStruct((spans, channels, tokens), BF16),
            jax.ShapeDtypeStruct((spans, tokens, 1), F32),
        ],
        compiler_params=pltpu.CompilerParams(vmem_limit_bytes=16 * 1024 * 1024),
        cost_estimate=pl.CostEstimate(
            flops=2 * spans * tokens * width * (channels + 8), bytes_accessed=5_000_000, transcendentals=0
        ),
    )(column.reshape(1), *parts, kind, gain, w_kv)


def sublayers(acts, grads_in, head_grads, types, gains, w_query, w_key, w_value):
    tensors = lax.axis_size("tensor")
    sections = lax.axis_size("section") // SUB
    place = lax.axis_index("section")
    position = place % SUB
    column = lax.axis_index("tensor")
    acts, grads_in, head_grads = acts[0], grads_in[0], head_grads[0]
    spans, tokq, cols = acts.shape
    tokens = tokq * SUB
    width = cols * tensors
    quarter = gains.shape[3]

    upper = column // 4
    pair = jnp.stack([acts, swapped(acts, "tensor", 4)])
    cols_all = in_quads(copies(pair, 4))
    cols_x = swapped(cols_all, "section", 2)
    x_parts = [cols_all, cols_x, swapped(cols_all, "section", 1), swapped(cols_x, "section", 1)]

    small = jnp.concatenate(
        [
            gains[0].reshape(spans, 2 * quarter),
            jnp.pad(types[0].astype(BF16), ((0, 0), (0, 128 - tokq))),
        ],
        axis=1,
    )
    small_x = swapped(small, "section", 2)
    small_pair = jnp.stack([small, small_x])
    small_core = swapped(small_pair, "section", 1)
    small_all = jnp.concatenate([small_pair, small_core])
    kind = jnp.transpose(small_all[:, :, 2 * quarter : 2 * quarter + tokq], (1, 0, 2))
    kind = kind.reshape(spans, tokens, 1).astype(F32)
    low_bit = position & 1 == 1
    high_bit = position & 2 == 2
    rates = small_all[:, :, : 2 * quarter].reshape(2, 2, spans, 2, quarter)
    rates = jnp.where(low_bit, rates[::-1], rates)
    rates = jnp.where(high_bit, rates[:, ::-1], rates)
    gain = jnp.transpose(rates, (2, 3, 1, 0, 4)).reshape(spans, 2, width).astype(F32)

    wq = w_query[0]
    w_kv = jnp.concatenate(
        [jnp.swapaxes(w_key[0], 1, 2), jnp.swapaxes(w_value[0], 1, 2)], axis=1
    )
    part = w_kv.shape[1]
    out_grads = blocks_by(head_grads, 1, SUB, position, ROW_MASKS)

    normed, kv_part, inverse = normalised(column, x_parts, kind, gain, w_kv)

    kv_all = exchanged(copies(kv_part, tensors))
    kv_all = jnp.transpose(
        kv_all.reshape(tensors, spans, 2, part // 2, tokens), (2, 1, 0, 3, 4)
    ).reshape(2, spans, HEAD_DIM, tokens)
    key_rows, value_rows = kv_all[0], kv_all[1]

    query_float = jnp.einsum("ntd,ndh->nth", normed, wq, preferred_element_type=F32)
    queries = query_float.astype(BF16)
    scale = HEAD_DIM ** (-0.5)
    index = jnp.concatenate([(position ^ m) * tokq + jnp.arange(tokq) for m in ROW_MASKS])
    causal = index[:, None] >= index[None, :]
    scores = jnp.einsum("nqh,nhk->nqk", queries, key_rows, preferred_element_type=F32) * scale
    scores = jnp.where(causal[None], scores, -1e30)
    probs = jax.nn.softmax(scores, axis=-1)
    probs_low = probs.astype(BF16)
    prob_grads = jnp.einsum("nqh,nhk->nqk", out_grads, value_rows, preferred_element_type=F32)
    score_grads = (
        probs * (prob_grads - jnp.sum(prob_grads * probs, axis=-1, keepdims=True)) * scale
    ).astype(BF16)
    key_each = jnp.einsum("nqk,nqh->nhk", score_grads, queries, preferred_element_type=F32)
    value_each = jnp.einsum("nqk,nqh->nhk", probs_low, out_grads, preferred_element_type=F32)
    query_grads = jnp.einsum(
        "nqk,nhk->nqh", score_grads, key_rows, preferred_element_type=F32
    ).astype(BF16)
    dots = jnp.sum(query_grads.astype(F32) * query_float, axis=2)
    dots = dots + jnp.sum(
        key_each * key_rows.astype(F32) + value_each * value_rows.astype(F32), axis=1
    )
    kv_sent = jnp.concatenate(
        [
            key_each.reshape(spans, tensors, part // 2, tokens),
            value_each.reshape(spans, tensors, part // 2, tokens),
            jnp.broadcast_to(dots[:, None, None], (spans, tensors, 8, tokens)),
        ],
        axis=2,
    ).astype(BF16)
    kv_came = exchanged(jnp.transpose(kv_sent, (1, 0, 2, 3)).astype(BF16))
    kv_sum = jnp.sum(kv_came.astype(F32), axis=0)
    kv_grads = kv_sum[:, :part].astype(BF16)
    dot_sum = kv_sum[:, part]
    half = tokens // 2

    def spread(rows):
        return jnp.einsum(
            "nth,ndh->ntd", query_grads[:, rows], wq, preferred_element_type=F32
        ) + jnp.einsum("nct,ncd->ntd", kv_grads[:, :, rows], w_kv, preferred_element_type=F32)

    came = swapped(spread(slice(half, None)).astype(BF16), "section", 1)
    total = spread(slice(0, half)) + came.astype(F32)
    middle = width // 2
    halves = [lax.dynamic_slice_in_dim(total, at * middle, middle, 2) for at in (1 - upper, upper)]
    low = [rows[:, tokq:].astype(BF16) for rows in halves]
    far_came = swapped(low[0], "section", 2)
    near_came = swapped(low[1], "section", 2)

    def summed(rows, came):
        mine = (rows[:, :tokq] + came.astype(F32)).astype(BF16)
        mine = jnp.stack([mine[:, :, i * cols : (i + 1) * cols] for i in range(4)])
        return jnp.sum(in_quads(mine).astype(F32), axis=0)

    far = summed(halves[0], far_came).astype(BF16)
    far, near_came = lax.optimization_barrier((far, near_came))
    far = swapped(far, "tensor", 4)
    grad_mine = summed(halves[1], near_came) + far.astype(F32)
    dot_pair = dot_sum[:, :half] + swapped(dot_sum[:, half:], "section", 1)
    dot_mine = dot_pair[:, :tokq] + swapped(dot_pair[:, tokq:], "section", 2)
    my_inverse = inverse[:, :tokq]
    my_gain = lax.dynamic_slice_in_dim(gain, column * cols, cols, 2)
    my_gain = jnp.where(kind[:, :tokq] > 0.5, my_gain[:, 1:2], my_gain[:, 0:1])
    stat = (dot_mine / width)[..., None]
    norm_grads = my_inverse * my_gain * grad_mine - acts.astype(F32) * my_inverse**2 * stat
    result = (grads_in.astype(F32) + norm_grads).astype(BF16)
    arrived = shifted(result, -SUB)
    routed = jnp.where(place // SUB == sections - 1, arrived[::-1], arrived)
    return routed[None]


def solution(mesh):
    return jax.shard_map(
        sublayers,
        mesh=mesh,
        in_specs=(
            P("section", None, None, "tensor"),
            P("section", None, None, "tensor"),
            P("section", None, None, "tensor"),
            P("section", None, None),
            P("section", None, None, None),
            P("section", None, None, "tensor"),
            P("section", None, None, "tensor"),
            P("section", None, None, "tensor"),
        ),
        out_specs=P("section", None, None, "tensor"),
        check_vma=False,
    )
```

time: 425 us -> 187 us (0.44)
  the two profiles are of different devices: /device:TPU:61 before, /device:TPU:2 now
where the time goes in v1:
time: 187 us; the launch traced here: 186 us
  starting transfers between devices  90.4 us (48%)
  waiting for transfers between devices  68.6 us (37%)
  matrix products  11.6 us (6%)
  other arithmetic  7.36 us (4%)
  local copies, waits for them, and re-layouts  4.37 us (2%)
  Pallas kernels  3.03 us (2%)
    ppermute x12, starting transfers between devices, swapped(): return lax.ppermute(value, axis, pairs)  42.5 us
    ppermute x12, waiting for transfers between devices, swapped(): return lax.ppermute(value, axis, pairs)  35.6 us
    all_to_all x2, waiting for transfers between devices, exchanged(): return lax.all_to_all(parts, 'tensor', 0, 0, tiled=True)  20 us
    ppermute x1, starting transfers between devices, shifted(): lax.ppermute(value, 'section', [(i, (i + by) % peers) for i in range(peer...  18.8 us
    all_to_all x3, starting transfers between devices, in_quads(): lax.all_to_all(parts, 'tensor', 0, 0, axis_index_groups=groups, tiled=True)  16.5 us
    all_to_all x2, starting transfers between devices, exchanged(): return lax.all_to_all(parts, 'tensor', 0, 0, tiled=True)  12.7 us
    all_to_all x3, waiting for transfers between devices, in_quads(): lax.all_to_all(parts, 'tensor', 0, 0, axis_index_groups=groups, tiled=True)  11.2 us
    dot_general x2, matrix products, spread(): jnp.einsum('nct,ncd->ntd', kv_grads[:, :, rows], w_kv, preferred_element_...  4.84 us
  transfers between devices with their start and end apart: 18, of which 15 were waited for; matrix products, arithmetic and copies ran while one was open for 5% of the time, Pallas kernels for 0%

profile of v1, /device:TPU:2, one launch (start us, length us, event | category | flops | bytes accessed | tf_op | source)
XLA Modules:
  0.0 186.0 jit_solution(3837310508652099846)
XLA Ops:
  0.0 11.0 %collective-permute-start = (bf16[2,32,512]{2,1,0:T(8,128)(2,1)}, bf16[2,32,512]{2,1,0:T(8,128)(2,1)S(1)}, u32[]{:S(2)}, u32[]{:S(2)}) collective-permute-start(bf16[2,32,512]{2,1,0:T(8,128)(2,1)} %bitcast.87), channel_id=1, source_target_pairs={{0,4},{1,5},{2,6},{3,7},{4,0},{5,1},{6,2},{7,3},{8,12},{9,13},{10,... | collective-permute-start | bytes 196616 | tf_op jit(solution)/shard_map/ppermute | solution.py:20
  11.0 0.7 copy.70
  11.8 1.7 collective-permute-done
  13.5 0.9 pad_maximum_fusion.3
  14.3 0.9 broadcast_in_dim.70
  15.2 8.2 %all-to-all-start = ((bf16[4,2,2,32,512]{4,3,2,1,0:T(8,128)(2,1)}), bf16[4,2,2,32,512]{4,3,2,1,0:T(8,128)(2,1)S(1)}, u32[]{:S(2)}, u32[]{:S(2)}) async-start(bf16[4,2,2,32,512]{4,3,2,1,0:T(8,128)(2,1)} %broadcast_in_dim.70), calls=%async_computation | async-start | bytes 1048576 | tf_op jit(solution)/shard_map/all_to_all | solution.py:38
  23.4 0.7 convert_bitcast_fusion.2
  24.1 7.3 %collective-permute-start.4 = (bf16[2,2176]{1,0:T(2,128)(2,1)S(1)}, bf16[2,2176]{1,0:T(2,128)(2,1)S(1)}, u32[]{:S(2)}, u32[]{:S(2)}) collective-permute-start(bf16[2,2176]{1,0:T(2,128)(2,1)S(1)} %fusion.38), channel_id=1, source_target_pairs={{0,16},{8,24},{16,0},{24,8},{32,48},{40,56},{48,32},{56,40},{64,80... | collective-permute-start | bytes 26120 | tf_op jit(solution)/shard_map/ppermute | solution.py:20
  31.4 1.1 pad_maximum_fusion.refs_6_
  32.5 5.4 %all-to-all-done.refs_0_ = bf16[4,2,2,32,512]{4,3,2,1,0:T(8,128)(2,1)S(1)} async-done(((bf16[4,2,2,32,512]{4,3,2,1,0:T(8,128)(2,1)}), bf16[4,2,2,32,512]{4,3,2,1,0:T(8,128)(2,1)S(1)}, u32[]{:S(2)}, u32[]{:S(2)}) %all-to-all-start) | async-done | bytes 524320 | tf_op jit(solution)/shard_map/all_to_all | solution.py:38
  37.9 3.0 %collective-permute-start.1 = (bf16[4,2,2,32,512]{4,3,2,1,0:T(8,128)(2,1)S(1)}, bf16[4,2,2,32,512]{4,3,2,1,0:T(8,128)(2,1)}, u32[]{:S(2)}, u32[]{:S(2)}) collective-permute-start(bf16[4,2,2,32,512]{4,3,2,1,0:T(8,128)(2,1)S(1)} %all-to-all-done.refs_0_), channel_id=1, source_target_pairs={{0,16},{8,24},{16,0},{24,8},{32,48},{40,56},{48,32},{56,40},{64,80... | collective-permute-start | bytes 1572872 | tf_op jit(solution)/shard_map/ppermute | solution.py:20
  40.9 1.9 %collective-permute-start.5 = (bf16[2,2,2176]{2,1,0:T(2,128)(2,1)S(1)}, bf16[2,2,2176]{2,1,0:T(2,128)(2,1)S(1)}, u32[]{:S(2)}, u32[]{:S(2)}) collective-permute-start(bf16[2,2,2176]{2,1,0:T(2,128)(2,1)S(1)} %pad_maximum_fusion.7), channel_id=1, source_target_pairs={{0,8},{8,0},{16,24},{24,16},{32,40},{40,32},{48,56},{56,48},{64,72... | collective-permute-start | bytes 52232 | tf_op jit(solution)/shard_map/ppermute | solution.py:20
  43.0 1.1 collective-permute-done.5
  44.1 2.1 %collective-permute-start.2 = (bf16[4,2,2,32,512]{4,3,2,1,0:T(8,128)(2,1)S(1)}, bf16[4,2,2,32,512]{4,3,2,1,0:T(8,128)(2,1)}, u32[]{:S(2)}, u32[]{:S(2)}) collective-permute-start(bf16[4,2,2,32,512]{4,3,2,1,0:T(8,128)(2,1)S(1)} %all-to-all-done.refs_0_), channel_id=1, source_target_pairs={{0,8},{8,0},{16,24},{24,16},{32,40},{40,32},{48,56},{56,48},{64,72... | collective-permute-start | bytes 1572872 | tf_op jit(solution)/shard_map/ppermute | solution.py:20
  46.2 6.6 %collective-permute-done.1.refs_1_ = bf16[4,2,2,32,512]{4,3,2,1,0:T(8,128)(2,1)} collective-permute-done((bf16[4,2,2,32,512]{4,3,2,1,0:T(8,128)(2,1)S(1)}, bf16[4,2,2,32,512]{4,3,2,1,0:T(8,128)(2,1)}, u32[]{:S(2)}, u32[]{:S(2)}) %collective-permute-start.1) | collective-permute-done | bytes 524320 | tf_op jit(solution)/shard_map/ppermute | solution.py:20
  52.8 1.9 %collective-permute-start.3 = (bf16[4,2,2,32,512]{4,3,2,1,0:T(8,128)(2,1)}, bf16[4,2,2,32,512]{4,3,2,1,0:T(8,128)(2,1)}, u32[]{:S(2)}, u32[]{:S(2)}) collective-permute-start(bf16[4,2,2,32,512]{4,3,2,1,0:T(8,128)(2,1)} %collective-permute-done.1.refs_1_), channel_id=1, source_target_pairs={{0,8},{8,0},{16,24},{24,16},{32,40},{40,32},{48,56},{56,48},{64,72... | collective-permute-start | bytes 1572872 | tf_op jit(solution)/shard_map/ppermute | solution.py:20
  54.9 0.1 reshape.92.refs_5_
  55.0 0.1 reshape.91
  55.1 0.1 copy.41.refs_4_
  55.2 1.7 collective-permute-done.3.refs_3_
  57.0 3.0 %shard_map.82 = (bf16[2,128,4096]{2,1,0:T(8,128)(2,1)S(1)}, bf16[2,32,128]{2,1,0:T(8,128)(2,1)S(1)}, f32[2,128,1]{2,1,0:T(8,128)S(1)}) custom-call(s32[1]{0:T(128)} %bitcast.1.column, bf16[4,2,2,32,512]{4,3,2,1,0:T(8,128)(2,1)S(1)} %all-to-all-done.refs_0_, bf16[4,2,2,32,512]{4,3,2,1,0:T(8,128)(2,1)} %collective-permute-done.1.refs_1_, ...), custom_call_target="tpu_custom_call" | custom-call | flops 83886080 | bytes 5000000 | tf_op jit(solution)/shard_map/pallas_call | solution.py:85
  60.0 1.3 copy-done.1
  61.3 0.7 broadcast_in_dim.78
  62.0 8.4 %all-to-all-start.1 = ((bf16[8,2,32,128]{3,2,1,0:T(8,128)(2,1)}), bf16[8,2,32,128]{3,2,1,0:T(8,128)(2,1)S(1)}, u32[]{:S(2)}, u32[]{:S(2)}) async-start(bf16[8,2,32,128]{3,2,1,0:T(8,128)(2,1)} %broadcast_in_dim.78), calls=%async_computation.1 | async-start | bytes 262144 | tf_op jit(solution)/shard_map/all_to_all | solution.py:42
  70.4 0.1 broadcast_compare_fusion
  70.5 2.5 %fusion.7 = f32[2,128,128]{1,2,0:T(8,128)S(1)} fusion(bf16[2,128,4096]{2,1,0:T(8,128)(2,1)} %copy-done.1, bf16[1,2,4096,128]{3,2,1,0:T(8,128)(2,1)S(1)} %copy-done), kind=kOutput, calls=%fused_computation.9 | convolution fusion | flops 268435456 | bytes 4325376 | tf_op jit(solution)/shard_map/ntd,ndh->nth/dot_general | solution.py:157
  73.1 9.6 %all-to-all-done.1 = bf16[8,2,32,128]{3,2,1,0:T(8,128)(2,1)S(1)} async-done(((bf16[8,2,32,128]{3,2,1,0:T(8,128)(2,1)}), bf16[8,2,32,128]{3,2,1,0:T(8,128)(2,1)S(1)}, u32[]{:S(2)}, u32[]{:S(2)}) %all-to-all-start.1) | async-done | bytes 131104 | tf_op jit(solution)/shard_map/all_to_all | solution.py:42
  82.6 0.2 fusion.12
  82.9 0.1 fusion.47
  83.0 0.2 fusion.27
  83.2 0.2 fusion.37
  83.5 0.2 multiply_reduce_fusion.1
  83.7 0.2 fusion.45
  83.9 0.7 maximum_bitcast_fusion
  84.6 4.3 %all-to-all-start.2 = ((bf16[8,2,40,128]{3,2,1,0:T(8,128)(2,1)}), bf16[8,2,40,128]{3,2,1,0:T(8,128)(2,1)S(1)}, u32[]{:S(2)}, u32[]{:S(2)}) async-start(bf16[8,2,40,128]{3,2,1,0:T(8,128)(2,1)} %maximum_bitcast_fusion), calls=%async_computation.2 | async-start | bytes 327680 | tf_op jit(solution)/shard_map/all_to_all | solution.py:42
  88.9 2.3 %fusion.3 = f32[2,64,4096]{2,1,0:T(8,128)} fusion(bf16[1,2,4096,128]{3,2,1,0:T(8,128)(2,1)S(1)} %copy-done, bf16[2,128,128]{1,2,0:T(8,128)(2,1)S(1)} %get-tuple-element.41), kind=kOutput, calls=%fused_computation.5 | convolution fusion | flops 134217728 | bytes 4259840 | tf_op jit(solution)/shard_map/nth,ndh->ntd/dot_general | solution.py:194
  91.2 10.4 %all-to-all-done.2 = bf16[8,2,40,128]{3,2,1,0:T(8,128)(2,1)S(1)} async-done(((bf16[8,2,40,128]{3,2,1,0:T(8,128)(2,1)}), bf16[8,2,40,128]{3,2,1,0:T(8,128)(2,1)S(1)}, u32[]{:S(2)}, u32[]{:S(2)}) %all-to-all-start.2) | async-done | bytes 163872 | tf_op jit(solution)/shard_map/all_to_all | solution.py:42
  101.7 3.1 %fusion.2 = bf16[2,64,4096]{2,1,0:T(8,128)(2,1)} fusion(f32[2,64,4096]{2,1,0:T(8,128)} %fusion.3, bf16[2,40,128]{2,1,0:T(8,128)(2,1)S(1)} %convert.30, bf16[2,16,4096]{2,1,0:T(8,128)(2,1)S(1)} %bitcast.81, bf16[2,16,4096]{2,1,0:T(8,128)(2,1)S(1)} %bitcast.84), kind=kOutput, calls=%fused_computation.4 | convolution fusion | flops 35651584 | bytes 3686400 | tf_op jit(solution)/shard_map/nct,ncd->ntd/dot_general | solution.py:196
  104.8 1.9 %collective-permute-start.6 = (bf16[2,64,4096]{2,1,0:T(8,128)(2,1)}, bf16[2,64,4096]{2,1,0:T(8,128)(2,1)}, u32[]{:S(2)}, u32[]{:S(2)}) collective-permute-start(bf16[2,64,4096]{2,1,0:T(8,128)(2,1)} %fusion.2), channel_id=1, source_target_pairs={{0,8},{8,0},{16,24},{24,16},{32,40},{40,32},{48,56},{56,48},{64,72... | collective-permute-start | bytes 3145736 | tf_op jit(solution)/shard_map/ppermute | solution.py:20
  106.7 0.9 fusion.5
  107.6 2.1 %collective-permute-done.6 = bf16[2,64,4096]{2,1,0:T(8,128)(2,1)} collective-permute-done((bf16[2,64,4096]{2,1,0:T(8,128)(2,1)}, bf16[2,64,4096]{2,1,0:T(8,128)(2,1)}, u32[]{:S(2)}, u32[]{:S(2)}) %collective-permute-start.6) | collective-permute-done | bytes 1048608 | tf_op jit(solution)/shard_map/ppermute | solution.py:20
  109.7 1.7 convert_add_fusion
  111.5 2.6 %collective-permute-start.7 = (bf16[2,32,2048]{2,1,0:T(8,128)(2,1)S(1)}, bf16[2,32,2048]{2,1,0:T(8,128)(2,1)S(1)}, u32[]{:S(2)}, u32[]{:S(2)}) collective-permute-start(bf16[2,32,2048]{2,1,0:T(8,128)(2,1)S(1)} %get-tuple-element.18), channel_id=1, source_target_pairs={{0,16},{8,24},{16,0},{24,8},{32,48},{40,56},{48,32},{56,40},{64,80... | collective-permute-start | bytes 786440 | tf_op jit(solution)/shard_map/ppermute | solution.py:20
  114.2 7.6 %collective-permute-done.7 = bf16[2,32,2048]{2,1,0:T(8,128)(2,1)S(1)} collective-permute-done((bf16[2,32,2048]{2,1,0:T(8,128)(2,1)S(1)}, bf16[2,32,2048]{2,1,0:T(8,128)(2,1)S(1)}, u32[]{:S(2)}, u32[]{:S(2)}) %collective-permute-start.7) | collective-permute-done | bytes 262176 | tf_op jit(solution)/shard_map/ppermute | solution.py:20
  121.8 0.7 pad_maximum_fusion.1
  122.6 3.5 %all-to-all-start.3 = ((bf16[4,2,32,512]{3,2,1,0:T(8,128)(2,1)}), bf16[4,2,32,512]{3,2,1,0:T(8,128)(2,1)S(1)}, u32[]{:S(2)}, u32[]{:S(2)}) async-start(bf16[4,2,32,512]{3,2,1,0:T(8,128)(2,1)} %pad_maximum_fusion.1), calls=%async_computation.3 | async-start | bytes 524288 | tf_op jit(solution)/shard_map/all_to_all | solution.py:38
  126.1 2.6 %collective-permute-start.8 = (bf16[2,32,2048]{2,1,0:T(8,128)(2,1)S(1)}, bf16[2,32,2048]{2,1,0:T(8,128)(2,1)S(1)}, u32[]{:S(2)}, u32[]{:S(2)}) collective-permute-start(bf16[2,32,2048]{2,1,0:T(8,128)(2,1)S(1)} %get-tuple-element.17), channel_id=1, source_target_pairs={{0,16},{8,24},{16,0},{24,8},{32,48},{40,56},{48,32},{56,40},{64,80... | collective-permute-start | bytes 786440 | tf_op jit(solution)/shard_map/ppermute | solution.py:20
  128.8 0.1 constant_dynamic-slice_fusion
  128.9 5.8 %all-to-all-done.3 = bf16[4,2,32,512]{3,2,1,0:T(8,128)(2,1)S(1)} async-done(((bf16[4,2,32,512]{3,2,1,0:T(8,128)(2,1)}), bf16[4,2,32,512]{3,2,1,0:T(8,128)(2,1)S(1)}, u32[]{:S(2)}, u32[]{:S(2)}) %all-to-all-start.3) | async-done | bytes 262176 | tf_op jit(solution)/shard_map/all_to_all | solution.py:38
  134.7 0.8 collective-permute-done.8
  135.5 1.1 fusion.18
  136.6 0.7 pad_maximum_fusion.2
  137.4 4.8 %all-to-all-start.4 = ((bf16[4,2,32,512]{3,2,1,0:T(8,128)(2,1)}), bf16[4,2,32,512]{3,2,1,0:T(8,128)(2,1)S(1)}, u32[]{:S(2)}, u32[]{:S(2)}) async-start(bf16[4,2,32,512]{3,2,1,0:T(8,128)(2,1)} %pad_maximum_fusion.2), calls=%async_computation.4 | async-start | bytes 524288 | tf_op jit(solution)/shard_map/all_to_all | solution.py:38
  142.2 1.9 %collective-permute-start.10 = (f32[2,64]{1,0:T(2,128)S(1)}, f32[2,64]{1,0:T(2,128)S(1)}, u32[]{:S(2)}, u32[]{:S(2)}) collective-permute-start(f32[2,64]{1,0:T(2,128)S(1)} %slice.121), channel_id=1, source_target_pairs={{0,8},{8,0},{16,24},{24,16},{32,40},{40,32},{48,56},{56,48},{64,72... | collective-permute-start | bytes 1544 | tf_op jit(solution)/shard_map/ppermute | solution.py:20
  144.1 1.1 collective-permute-done.10
  145.3 2.6 %collective-permute-start.11 = (f32[2,32]{1,0:T(2,128)S(1)}, f32[2,32]{1,0:T(2,128)S(1)}, u32[]{:S(2)}, u32[]{:S(2)}) collective-permute-start(f32[2,32]{1,0:T(2,128)S(1)} %slice.123), channel_id=1, source_target_pairs={{0,16},{8,24},{16,0},{24,8},{32,48},{40,56},{48,32},{56,40},{64,80... | collective-permute-start | bytes 776 | tf_op jit(solution)/shard_map/ppermute | solution.py:20
  148.0 0.1 slice_reduce_fusion
  148.1 2.7 %collective-permute-done.11 = f32[2,32]{1,0:T(2,128)S(1)} collective-permute-done((f32[2,32]{1,0:T(2,128)S(1)}, f32[2,32]{1,0:T(2,128)S(1)}, u32[]{:S(2)}, u32[]{:S(2)}) %collective-permute-start.11) | collective-permute-done | bytes 288 | tf_op jit(solution)/shard_map/ppermute | solution.py:20
  150.8 3.5 %collective-permute-start.9 = (bf16[2,32,512]{2,1,0:T(8,128)(2,1)S(1)}, bf16[2,32,512]{2,1,0:T(8,128)(2,1)S(1)}, u32[]{:S(2)}, u32[]{:S(2)}) collective-permute-start(bf16[2,32,512]{2,1,0:T(8,128)(2,1)S(1)} %reduce_sum.71), channel_id=1, source_target_pairs={{0,4},{1,5},{2,6},{3,7},{4,0},{5,1},{6,2},{7,3},{8,12},{9,13},{10,... | collective-permute-start | bytes 196616 | tf_op jit(solution)/shard_map/ppermute | solution.py:20
  154.4 10.2 %collective-permute-done.9 = bf16[2,32,512]{2,1,0:T(8,128)(2,1)S(1)} collective-permute-done((bf16[2,32,512]{2,1,0:T(8,128)(2,1)S(1)}, bf16[2,32,512]{2,1,0:T(8,128)(2,1)S(1)}, u32[]{:S(2)}, u32[]{:S(2)}) %collective-permute-start.9) | collective-permute-done | bytes 65568 | tf_op jit(solution)/shard_map/ppermute | solution.py:20
  164.6 0.1 fusion.23
  164.7 18.8 %collective-permute-start.12 = (bf16[2,32,512]{2,1,0:T(8,128)(2,1)S(1)}, bf16[2,32,512]{2,1,0:T(8,128)(2,1)S(1)}, u32[]{:S(2)}, u32[]{:S(2)}) collective-permute-start(bf16[2,32,512]{2,1,0:T(8,128)(2,1)S(1)} %fusion.23), channel_id=1, source_target_pairs={{0,992},{8,1000},{16,1008},{24,1016},{32,0},{40,8},{48,16},{56,24}... | collective-permute-start | bytes 196616 | tf_op jit(solution)/shard_map/ppermute | solution.py:25
  183.5 1.9 %collective-permute-done.12 = bf16[2,32,512]{2,1,0:T(8,128)(2,1)S(1)} collective-permute-done((bf16[2,32,512]{2,1,0:T(8,128)(2,1)S(1)}, bf16[2,32,512]{2,1,0:T(8,128)(2,1)S(1)}, u32[]{:S(2)}, u32[]{:S(2)}) %collective-permute-start.12) | collective-permute-done | bytes 65568 | tf_op jit(solution)/shard_map/ppermute | solution.py:25
  185.4 0.6 fusion.24
  (52 shorter events, 0.9 us)
Async XLA Ops:
  0.0 70.5 %copy-start = (bf16[1,2,4096,128]{3,2,1,0:T(8,128)(2,1)S(1)}, bf16[1,2,4096,128]{3,2,1,0:T(8,128)(2,1)}, u32[]{:S(2)}) copy-start(bf16[1,2,4096,128]{3,2,1,0:T(8,128)(2,1)} %param.13) | copy-start | bytes 6291460
  0.0 13.5 %collective-permute-start = (bf16[2,32,512]{2,1,0:T(8,128)(2,1)}, bf16[2,32,512]{2,1,0:T(8,128)(2,1)S(1)}, u32[]{:S(2)}, u32[]{:S(2)}) collective-permute-start(bf16[2,32,512]{2,1,0:T(8,128)(2,1)} %bitcast.87), channel_id=1, source_target_pairs={{0,4},{1,5},{2,6},{3,7},{4,0},{5,1},{6,2},{7,3},{8,12},{9,13},{10,... | collective-permute-start | bytes 196616 | tf_op jit(solution)/shard_map/ppermute | solution.py:20
  15.2 22.7 %all-to-all-start = ((bf16[4,2,2,32,512]{4,3,2,1,0:T(8,128)(2,1)}), bf16[4,2,2,32,512]{4,3,2,1,0:T(8,128)(2,1)S(1)}, u32[]{:S(2)}, u32[]{:S(2)}) async-start(bf16[4,2,2,32,512]{4,3,2,1,0:T(8,128)(2,1)} %broadcast_in_dim.70), calls=%async_computation | async-start | bytes 1048576 | tf_op jit(solution)/shard_map/all_to_all | solution.py:38
  24.1 16.9 %collective-permute-start.4 = (bf16[2,2176]{1,0:T(2,128)(2,1)S(1)}, bf16[2,2176]{1,0:T(2,128)(2,1)S(1)}, u32[]{:S(2)}, u32[]{:S(2)}) collective-permute-start(bf16[2,2176]{1,0:T(2,128)(2,1)S(1)} %fusion.38), channel_id=1, source_target_pairs={{0,16},{8,24},{16,0},{24,8},{32,48},{40,56},{48,32},{56,40},{64,80... | collective-permute-start | bytes 26120 | tf_op jit(solution)/shard_map/ppermute | solution.py:20
  32.5 38.0 %copy-start.7 = (bf16[1,2,128,128]{3,2,1,0:T(8,128)(2,1)S(1)}, bf16[1,2,128,128]{3,2,1,0:T(8,128)(2,1)}, u32[]{:S(2)}) copy-start(bf16[1,2,128,128]{3,2,1,0:T(8,128)(2,1)} %param.10) | copy-start | bytes 196612
  37.9 14.9 %collective-permute-start.1 = (bf16[4,2,2,32,512]{4,3,2,1,0:T(8,128)(2,1)S(1)}, bf16[4,2,2,32,512]{4,3,2,1,0:T(8,128)(2,1)}, u32[]{:S(2)}, u32[]{:S(2)}) collective-permute-start(bf16[4,2,2,32,512]{4,3,2,1,0:T(8,128)(2,1)S(1)} %all-to-all-done.refs_0_), channel_id=1, source_target_pairs={{0,16},{8,24},{16,0},{24,8},{32,48},{40,56},{48,32},{56,40},{64,80... | collective-permute-start | bytes 1572872 | tf_op jit(solution)/shard_map/ppermute | solution.py:20
  40.9 3.1 %collective-permute-start.5 = (bf16[2,2,2176]{2,1,0:T(2,128)(2,1)S(1)}, bf16[2,2,2176]{2,1,0:T(2,128)(2,1)S(1)}, u32[]{:S(2)}, u32[]{:S(2)}) collective-permute-start(bf16[2,2,2176]{2,1,0:T(2,128)(2,1)S(1)} %pad_maximum_fusion.7), channel_id=1, source_target_pairs={{0,8},{8,0},{16,24},{24,16},{32,40},{40,32},{48,56},{56,48},{64,72... | collective-permute-start | bytes 52232 | tf_op jit(solution)/shard_map/ppermute | solution.py:20
  44.1 11.1 %collective-permute-start.2 = (bf16[4,2,2,32,512]{4,3,2,1,0:T(8,128)(2,1)S(1)}, bf16[4,2,2,32,512]{4,3,2,1,0:T(8,128)(2,1)}, u32[]{:S(2)}, u32[]{:S(2)}) collective-permute-start(bf16[4,2,2,32,512]{4,3,2,1,0:T(8,128)(2,1)S(1)} %all-to-all-done.refs_0_), channel_id=1, source_target_pairs={{0,8},{8,0},{16,24},{24,16},{32,40},{40,32},{48,56},{56,48},{64,72... | collective-permute-start | bytes 1572872 | tf_op jit(solution)/shard_map/ppermute | solution.py:20
  52.8 4.1 %collective-permute-start.3 = (bf16[4,2,2,32,512]{4,3,2,1,0:T(8,128)(2,1)}, bf16[4,2,2,32,512]{4,3,2,1,0:T(8,128)(2,1)}, u32[]{:S(2)}, u32[]{:S(2)}) collective-permute-start(bf16[4,2,2,32,512]{4,3,2,1,0:T(8,128)(2,1)} %collective-permute-done.1.refs_1_), channel_id=1, source_target_pairs={{0,8},{8,0},{16,24},{24,16},{32,40},{40,32},{48,56},{56,48},{64,72... | collective-permute-start | bytes 1572872 | tf_op jit(solution)/shard_map/ppermute | solution.py:20
  60.0 1.3 copy-start.1
  62.0 20.6 %all-to-all-start.1 = ((bf16[8,2,32,128]{3,2,1,0:T(8,128)(2,1)}), bf16[8,2,32,128]{3,2,1,0:T(8,128)(2,1)S(1)}, u32[]{:S(2)}, u32[]{:S(2)}) async-start(bf16[8,2,32,128]{3,2,1,0:T(8,128)(2,1)} %broadcast_in_dim.78), calls=%async_computation.1 | async-start | bytes 262144 | tf_op jit(solution)/shard_map/all_to_all | solution.py:42
  84.6 17.0 %all-to-all-start.2 = ((bf16[8,2,40,128]{3,2,1,0:T(8,128)(2,1)}), bf16[8,2,40,128]{3,2,1,0:T(8,128)(2,1)S(1)}, u32[]{:S(2)}, u32[]{:S(2)}) async-start(bf16[8,2,40,128]{3,2,1,0:T(8,128)(2,1)} %maximum_bitcast_fusion), calls=%async_computation.2 | async-start | bytes 327680 | tf_op jit(solution)/shard_map/all_to_all | solution.py:42
  88.9 12.7 %copy-start.3 = (bf16[1,2,4096,16]{2,3,1,0:T(8,128)(2,1)S(1)}, bf16[1,2,4096,16]{2,3,1,0:T(8,128)(2,1)}, u32[]{:S(2)}) copy-start(bf16[1,2,4096,16]{2,3,1,0:T(8,128)(2,1)} %param.15) | copy-start | bytes 786436
  88.9 12.7 %copy-start.4 = (bf16[1,2,4096,16]{2,3,1,0:T(8,128)(2,1)S(1)}, bf16[1,2,4096,16]{2,3,1,0:T(8,128)(2,1)}, u32[]{:S(2)}) copy-start(bf16[1,2,4096,16]{2,3,1,0:T(8,128)(2,1)} %param.14) | copy-start | bytes 786436
  104.8 4.9 %collective-permute-start.6 = (bf16[2,64,4096]{2,1,0:T(8,128)(2,1)}, bf16[2,64,4096]{2,1,0:T(8,128)(2,1)}, u32[]{:S(2)}, u32[]{:S(2)}) collective-permute-start(bf16[2,64,4096]{2,1,0:T(8,128)(2,1)} %fusion.2), channel_id=1, source_target_pairs={{0,8},{8,0},{16,24},{24,16},{32,40},{40,32},{48,56},{56,48},{64,72... | collective-permute-start | bytes 3145736 | tf_op jit(solution)/shard_map/ppermute | solution.py:20
  111.4 10.3 %copy-start.2 = (f32[2,64,4096]{2,1,0:T(8,128)}, f32[2,64,4096]{2,1,0:T(8,128)S(1)}, u32[]{:S(2)}) copy-start(f32[2,64,4096]{2,1,0:T(8,128)S(1)} %convert_add_fusion) | copy-start | bytes 6291460
  111.5 10.2 %collective-permute-start.7 = (bf16[2,32,2048]{2,1,0:T(8,128)(2,1)S(1)}, bf16[2,32,2048]{2,1,0:T(8,128)(2,1)S(1)}, u32[]{:S(2)}, u32[]{:S(2)}) collective-permute-start(bf16[2,32,2048]{2,1,0:T(8,128)(2,1)S(1)} %get-tuple-element.18), channel_id=1, source_target_pairs={{0,16},{8,24},{16,0},{24,8},{32,48},{40,56},{48,32},{56,40},{64,80... | collective-permute-start | bytes 786440 | tf_op jit(solution)/shard_map/ppermute | solution.py:20
  122.6 42.0 %copy-start.5 = (bf16[1,2,32,512]{3,2,1,0:T(8,128)(2,1)S(1)}, bf16[1,2,32,512]{3,2,1,0:T(8,128)(2,1)}, u32[]{:S(2)}) copy-start(bf16[1,2,32,512]{3,2,1,0:T(8,128)(2,1)} %param.8) | copy-start | bytes 196612
  122.6 42.0 %copy-start.6 = (bf16[1,2,32,512]{3,2,1,0:T(8,128)(2,1)S(1)}, bf16[1,2,32,512]{3,2,1,0:T(8,128)(2,1)}, u32[]{:S(2)}) copy-start(bf16[1,2,32,512]{3,2,1,0:T(8,128)(2,1)} %param.9) | copy-start | bytes 196612
  122.6 12.1 %all-to-all-start.3 = ((bf16[4,2,32,512]{3,2,1,0:T(8,128)(2,1)}), bf16[4,2,32,512]{3,2,1,0:T(8,128)(2,1)S(1)}, u32[]{:S(2)}, u32[]{:S(2)}) async-start(bf16[4,2,32,512]{3,2,1,0:T(8,128)(2,1)} %pad_maximum_fusion.1), calls=%async_computation.3 | async-start | bytes 524288 | tf_op jit(solution)/shard_map/all_to_all | solution.py:38
  126.1 9.4 %collective-permute-start.8 = (bf16[2,32,2048]{2,1,0:T(8,128)(2,1)S(1)}, bf16[2,32,2048]{2,1,0:T(8,128)(2,1)S(1)}, u32[]{:S(2)}, u32[]{:S(2)}) collective-permute-start(bf16[2,32,2048]{2,1,0:T(8,128)(2,1)S(1)} %get-tuple-element.17), channel_id=1, source_target_pairs={{0,16},{8,24},{16,0},{24,8},{32,48},{40,56},{48,32},{56,40},{64,80... | collective-permute-start | bytes 786440 | tf_op jit(solution)/shard_map/ppermute | solution.py:20
  137.4 16.9 %all-to-all-start.4 = ((bf16[4,2,32,512]{3,2,1,0:T(8,128)(2,1)}), bf16[4,2,32,512]{3,2,1,0:T(8,128)(2,1)S(1)}, u32[]{:S(2)}, u32[]{:S(2)}) async-start(bf16[4,2,32,512]{3,2,1,0:T(8,128)(2,1)} %pad_maximum_fusion.2), calls=%async_computation.4 | async-start | bytes 524288 | tf_op jit(solution)/shard_map/all_to_all | solution.py:38
  142.2 3.0 %collective-permute-start.10 = (f32[2,64]{1,0:T(2,128)S(1)}, f32[2,64]{1,0:T(2,128)S(1)}, u32[]{:S(2)}, u32[]{:S(2)}) collective-permute-start(f32[2,64]{1,0:T(2,128)S(1)} %slice.121), channel_id=1, source_target_pairs={{0,8},{8,0},{16,24},{24,16},{32,40},{40,32},{48,56},{56,48},{64,72... | collective-permute-start | bytes 1544 | tf_op jit(solution)/shard_map/ppermute | solution.py:20
  145.3 5.5 %collective-permute-start.11 = (f32[2,32]{1,0:T(2,128)S(1)}, f32[2,32]{1,0:T(2,128)S(1)}, u32[]{:S(2)}, u32[]{:S(2)}) collective-permute-start(f32[2,32]{1,0:T(2,128)S(1)} %slice.123), channel_id=1, source_target_pairs={{0,16},{8,24},{16,0},{24,8},{32,48},{40,56},{48,32},{56,40},{64,80... | collective-permute-start | bytes 776 | tf_op jit(solution)/shard_map/ppermute | solution.py:20
  150.8 13.8 %collective-permute-start.9 = (bf16[2,32,512]{2,1,0:T(8,128)(2,1)S(1)}, bf16[2,32,512]{2,1,0:T(8,128)(2,1)S(1)}, u32[]{:S(2)}, u32[]{:S(2)}) collective-permute-start(bf16[2,32,512]{2,1,0:T(8,128)(2,1)S(1)} %reduce_sum.71), channel_id=1, source_target_pairs={{0,4},{1,5},{2,6},{3,7},{4,0},{5,1},{6,2},{7,3},{8,12},{9,13},{10,... | collective-permute-start | bytes 196616 | tf_op jit(solution)/shard_map/ppermute | solution.py:20
  164.7 20.7 %collective-permute-start.12 = (bf16[2,32,512]{2,1,0:T(8,128)(2,1)S(1)}, bf16[2,32,512]{2,1,0:T(8,128)(2,1)S(1)}, u32[]{:S(2)}, u32[]{:S(2)}) collective-permute-start(bf16[2,32,512]{2,1,0:T(8,128)(2,1)S(1)} %fusion.23), channel_id=1, source_target_pairs={{0,992},{8,1000},{16,1008},{24,1016},{32,0},{40,8},{48,16},{56,24}... | collective-permute-start | bytes 196616 | tf_op jit(solution)/shard_map/ppermute | solution.py:25

commit v2 on v1

--- a/solution.py
+++ b/solution.py
@@ -47,7 +47,7 @@
 
 
 def norm_kernel(column, *refs):
-    parts, (kind, gain, w_kv, normed, kv, inverse) = refs[:SUB], refs[SUB:]
+    parts, (kind, gain, w_query, w_kv, query, kv, inverse, normed) = refs[:SUB], refs[SUB:]
     quads, halves, _, rows, cols = parts[0].shape
     width = quads * halves * cols
     upper = column[0] // quads
@@ -66,13 +66,14 @@
                 block = (upper ^ h) * quads + i
                 at = pl.ds(pl.multiple_of(block * cols, cols), cols)
                 rates = jnp.where(speech, gain[0, 1:2, at], gain[0, 0:1, at])
-                normed[0, at_rows, at] = (part[i, h, 0].astype(F32) * inv * rates).astype(BF16)
+                normed[at_rows, at] = (part[i, h, 0].astype(F32) * inv * rates).astype(BF16)
     kv[0] = lax.dot_general(
-        w_kv[0], normed[0], (((1,), (1,)), ((), ())), preferred_element_type=F32
-    ).astype(BF16)
-
-
-def normalised(column, parts, kind, gain, w_kv):
+        w_kv[0], normed[...], (((1,), (1,)), ((), ())), preferred_element_type=F32
+    ).astype(BF16)
+    query[0] = jnp.dot(normed[...], w_query[0], preferred_element_type=F32)
+
+
+def projected(column, parts, kind, gain, w_query, w_kv):
     quads, halves, spans, rows, cols = parts[0].shape
     tokens = SUB * rows
     width = quads * halves * cols
@@ -87,18 +88,19 @@
         grid=(spans,),
         in_specs=[pl.BlockSpec(memory_space=pltpu.SMEM)]
         + [x_spec] * SUB
-        + [whole(tokens, 1), whole(2, width), whole(channels, width)],
-        out_specs=[whole(tokens, width), whole(channels, tokens), whole(tokens, 1)],
+        + [whole(tokens, 1), whole(2, width), whole(width, HEAD_DIM), whole(channels, width)],
+        out_specs=[whole(tokens, HEAD_DIM), whole(channels, tokens), whole(tokens, 1)],
         out_shape=[
-            jax.ShapeDtypeStruct((spans, tokens, width), BF16),
+            jax.ShapeDtypeStruct((spans, tokens, HEAD_DIM), F32),
             jax.ShapeDtypeStruct((spans, channels, tokens), BF16),
             jax.ShapeDtypeStruct((spans, tokens, 1), F32),
         ],
-        compiler_params=pltpu.CompilerParams(vmem_limit_bytes=16 * 1024 * 1024),
+        scratch_shapes=[pltpu.VMEM((tokens, width), BF16)],
+        compiler_params=pltpu.CompilerParams(vmem_limit_bytes=20 * 1024 * 1024),
         cost_estimate=pl.CostEstimate(
-            flops=2 * spans * tokens * width * (channels + 8), bytes_accessed=5_000_000, transcendentals=0
+            flops=2 * spans * tokens * width * (channels + HEAD_DIM), bytes_accessed=5_000_000, transcendentals=0
         ),
-    )(column.reshape(1), *parts, kind, gain, w_kv)
+    )(column.reshape(1), *parts, kind, gain, w_query, w_kv)
 
 
 def sublayers(acts, grads_in, head_grads, types, gains, w_query, w_key, w_value):
@@ -114,8 +116,12 @@
     quarter = gains.shape[3]
 
     upper = column // 4
-    pair = jnp.stack([acts, swapped(acts, "tensor", 4)])
-    cols_all = in_quads(copies(pair, 4))
+    across = swapped(acts, "tensor", 4)
+    shape = (4, 1, *acts.shape)
+    cols_all = jnp.concatenate(
+        [jnp.broadcast_to(acts, shape), jnp.broadcast_to(across, shape)], axis=1
+    )
+    cols_all = in_quads(cols_all)
     cols_x = swapped(cols_all, "section", 2)
     x_parts = [cols_all, cols_x, swapped(cols_all, "section", 1), swapped(cols_x, "section", 1)]
 
@@ -146,7 +152,7 @@
     part = w_kv.shape[1]
     out_grads = blocks_by(head_grads, 1, SUB, position, ROW_MASKS)
 
-    normed, kv_part, inverse = normalised(column, x_parts, kind, gain, w_kv)
+    query_float, kv_part, inverse = projected(column, x_parts, kind, gain, wq, w_kv)
 
     kv_all = exchanged(copies(kv_part, tensors))
     kv_all = jnp.transpose(
@@ -154,7 +160,6 @@
     ).reshape(2, spans, HEAD_DIM, tokens)
     key_rows, value_rows = kv_all[0], kv_all[1]
 
-    query_float = jnp.einsum("ntd,ndh->nth", normed, wq, preferred_element_type=F32)
     queries = query_float.astype(BF16)
     scale = HEAD_DIM ** (-0.5)
     index = jnp.concatenate([(position ^ m) * tokq + jnp.arange(tokq) for m in ROW_MASKS])

time: 187 us -> 186 us (level)
  waiting for transfers between devices: 68.6 us -> 72 us
  matrix products: 11.6 us -> 9.12 us
    all_to_all x2, waiting for transfers between devices: 20 us -> 22.5 us  [exchanged(): return lax.all_to_all(parts, 'tensor', 0, 0, tiled=True)]
    dot_general x1 -> x0, matrix products: 2.51 us -> none  [sublayers(): jnp.einsum('ntd,ndh->nth', normed, wq, preferred_element_type=F32)]
  transfers between devices with their start and end apart: 18 -> 18, of which waited for: 15 -> 15; matrix products, arithmetic and copies ran while one was open for 5% -> 3% of each run, Pallas kernels for 0% -> 0%
where the time goes in v2:
time: 186 us; the launch traced here: 185 us
  starting transfers between devices  90.4 us (49%)
  waiting for transfers between devices  72 us (39%)
  matrix products  9.12 us (5%)
  other arithmetic  6.3 us (3%)
  Pallas kernels  3.52 us (2%)
  local copies, waits for them, and re-layouts  2.97 us (2%)
    ppermute x12, starting transfers between devices, swapped(): return lax.ppermute(value, axis, pairs)  42.5 us
    ppermute x12, waiting for transfers between devices, swapped(): return lax.ppermute(value, axis, pairs)  35.7 us
    all_to_all x2, waiting for transfers between devices, exchanged(): return lax.all_to_all(parts, 'tensor', 0, 0, tiled=True)  22.5 us
    ppermute x1, starting transfers between devices, shifted(): lax.ppermute(value, 'section', [(i, (i + by) % peers) for i in range(peer...  18.8 us
    all_to_all x3, starting transfers between devices, in_quads(): lax.all_to_all(parts, 'tensor', 0, 0, axis_index_groups=groups, tiled=True)  16.5 us
    all_to_all x2, starting transfers between devices, exchanged(): return lax.all_to_all(parts, 'tensor', 0, 0, tiled=True)  12.7 us
    all_to_all x3, waiting for transfers between devices, in_quads(): lax.all_to_all(parts, 'tensor', 0, 0, axis_index_groups=groups, tiled=True)  11.9 us
    dot_general x2, matrix products, spread(): jnp.einsum('nct,ncd->ntd', kv_grads[:, :, rows], w_kv, preferred_element_...  4.85 us
  transfers between devices with their start and end apart: 18, of which 15 were waited for; matrix products, arithmetic and copies ran while one was open for 3% of the time, Pallas kernels for 0%

profile of v2, /device:TPU:2, one launch (start us, length us, event | category | flops | bytes accessed | tf_op | source)
XLA Modules:
  0.0 185.0 jit_solution(5837691005216953421)
XLA Ops:
  0.0 11.1 %collective-permute-start = (bf16[2,32,512]{2,1,0:T(8,128)(2,1)}, bf16[2,32,512]{2,1,0:T(8,128)(2,1)S(1)}, u32[]{:S(2)}, u32[]{:S(2)}) collective-permute-start(bf16[2,32,512]{2,1,0:T(8,128)(2,1)} %bitcast.84), channel_id=1, source_target_pairs={{0,4},{1,5},{2,6},{3,7},{4,0},{5,1},{6,2},{7,3},{8,12},{9,13},{10,... | collective-permute-start | bytes 196616 | tf_op jit(solution)/shard_map/ppermute | solution.py:20
  11.1 2.4 %collective-permute-done = bf16[2,32,512]{2,1,0:T(8,128)(2,1)S(1)} collective-permute-done((bf16[2,32,512]{2,1,0:T(8,128)(2,1)}, bf16[2,32,512]{2,1,0:T(8,128)(2,1)S(1)}, u32[]{:S(2)}, u32[]{:S(2)}) %collective-permute-start) | collective-permute-done | bytes 65568 | tf_op jit(solution)/shard_map/ppermute | solution.py:20
  13.5 0.9 broadcast_in_dim.70
  14.4 0.8 pad_maximum_fusion
  15.2 8.2 %all-to-all-start = ((bf16[4,2,2,32,512]{4,3,2,1,0:T(8,128)(2,1)}), bf16[4,2,2,32,512]{4,3,2,1,0:T(8,128)(2,1)S(1)}, u32[]{:S(2)}, u32[]{:S(2)}) async-start(bf16[4,2,2,32,512]{4,3,2,1,0:T(8,128)(2,1)} %pad_maximum_fusion), calls=%async_computation | async-start | bytes 1048576 | tf_op jit(solution)/shard_map/all_to_all | solution.py:38
  23.5 7.3 %collective-permute-start.4 = (bf16[2,2176]{1,0:T(2,128)(2,1)S(1)}, bf16[2,2176]{1,0:T(2,128)(2,1)S(1)}, u32[]{:S(2)}, u32[]{:S(2)}) collective-permute-start(bf16[2,2176]{1,0:T(2,128)(2,1)S(1)} %fusion.34), channel_id=1, source_target_pairs={{0,16},{8,24},{16,0},{24,8},{32,48},{40,56},{48,32},{56,40},{64,80... | collective-permute-start | bytes 26120 | tf_op jit(solution)/shard_map/ppermute | solution.py:20
  30.8 1.0 pad_maximum_fusion.1.refs_7_
  31.8 6.1 %all-to-all-done.refs_0_ = bf16[4,2,2,32,512]{4,3,2,1,0:T(8,128)(2,1)S(1)} async-done(((bf16[4,2,2,32,512]{4,3,2,1,0:T(8,128)(2,1)}), bf16[4,2,2,32,512]{4,3,2,1,0:T(8,128)(2,1)S(1)}, u32[]{:S(2)}, u32[]{:S(2)}) %all-to-all-start) | async-done | bytes 524320 | tf_op jit(solution)/shard_map/all_to_all | solution.py:38
  37.9 3.0 %collective-permute-start.1 = (bf16[4,2,2,32,512]{4,3,2,1,0:T(8,128)(2,1)S(1)}, bf16[4,2,2,32,512]{4,3,2,1,0:T(8,128)(2,1)}, u32[]{:S(2)}, u32[]{:S(2)}) collective-permute-start(bf16[4,2,2,32,512]{4,3,2,1,0:T(8,128)(2,1)S(1)} %all-to-all-done.refs_0_), channel_id=1, source_target_pairs={{0,16},{8,24},{16,0},{24,8},{32,48},{40,56},{48,32},{56,40},{64,80... | collective-permute-start | bytes 1572872 | tf_op jit(solution)/shard_map/ppermute | solution.py:20
  41.0 1.9 %collective-permute-start.5 = (bf16[2,2,2176]{2,1,0:T(2,128)(2,1)S(1)}, bf16[2,2,2176]{2,1,0:T(2,128)(2,1)S(1)}, u32[]{:S(2)}, u32[]{:S(2)}) collective-permute-start(bf16[2,2,2176]{2,1,0:T(2,128)(2,1)S(1)} %pad_maximum_fusion.7), channel_id=1, source_target_pairs={{0,8},{8,0},{16,24},{24,16},{32,40},{40,32},{48,56},{56,48},{64,72... | collective-permute-start | bytes 52232 | tf_op jit(solution)/shard_map/ppermute | solution.py:20
  42.9 1.1 collective-permute-done.5
  44.1 2.1 %collective-permute-start.2 = (bf16[4,2,2,32,512]{4,3,2,1,0:T(8,128)(2,1)S(1)}, bf16[4,2,2,32,512]{4,3,2,1,0:T(8,128)(2,1)}, u32[]{:S(2)}, u32[]{:S(2)}) collective-permute-start(bf16[4,2,2,32,512]{4,3,2,1,0:T(8,128)(2,1)S(1)} %all-to-all-done.refs_0_), channel_id=1, source_target_pairs={{0,8},{8,0},{16,24},{24,16},{32,40},{40,32},{48,56},{56,48},{64,72... | collective-permute-start | bytes 1572872 | tf_op jit(solution)/shard_map/ppermute | solution.py:20
  46.2 6.7 %collective-permute-done.1.refs_1_ = bf16[4,2,2,32,512]{4,3,2,1,0:T(8,128)(2,1)} collective-permute-done((bf16[4,2,2,32,512]{4,3,2,1,0:T(8,128)(2,1)S(1)}, bf16[4,2,2,32,512]{4,3,2,1,0:T(8,128)(2,1)}, u32[]{:S(2)}, u32[]{:S(2)}) %collective-permute-start.1) | collective-permute-done | bytes 524320 | tf_op jit(solution)/shard_map/ppermute | solution.py:20
  52.9 1.9 %collective-permute-start.3 = (bf16[4,2,2,32,512]{4,3,2,1,0:T(8,128)(2,1)}, bf16[4,2,2,32,512]{4,3,2,1,0:T(8,128)(2,1)}, u32[]{:S(2)}, u32[]{:S(2)}) collective-permute-start(bf16[4,2,2,32,512]{4,3,2,1,0:T(8,128)(2,1)} %collective-permute-done.1.refs_1_), channel_id=1, source_target_pairs={{0,8},{8,0},{16,24},{24,16},{32,40},{40,32},{48,56},{56,48},{64,72... | collective-permute-start | bytes 1572872 | tf_op jit(solution)/shard_map/ppermute | solution.py:20
  54.8 0.1 reshape.90
  55.0 0.1 reshape.91.refs_5_
  55.1 0.1 copy.33.refs_4_
  55.3 1.7 collective-permute-done.3.refs_3_
  57.0 3.5 %shard_map.82 = (f32[2,128,128]{2,1,0:T(8,128)S(1)}, bf16[2,32,128]{2,1,0:T(8,128)(2,1)S(1)}, f32[2,128,1]{2,1,0:T(8,128)S(1)}) custom-call(s32[1]{0:T(128)} %bitcast.1.column, bf16[4,2,2,32,512]{4,3,2,1,0:T(8,128)(2,1)S(1)} %all-to-all-done.refs_0_, bf16[4,2,2,32,512]{4,3,2,1,0:T(8,128)(2,1)} %collective-permute-done.1.refs_1_, ...), custom_call_target="tpu_custom_call" | custom-call | flops 335544320 | bytes 5000000 | tf_op jit(solution)/shard_map/pallas_call | solution.py:86
  60.5 0.6 copy-done.1
  61.2 0.7 broadcast_in_dim.79
  61.8 8.4 %all-to-all-start.1 = ((bf16[8,2,32,128]{3,2,1,0:T(8,128)(2,1)}), bf16[8,2,32,128]{3,2,1,0:T(8,128)(2,1)S(1)}, u32[]{:S(2)}, u32[]{:S(2)}) async-start(bf16[8,2,32,128]{3,2,1,0:T(8,128)(2,1)} %broadcast_in_dim.79), calls=%async_computation.1 | async-start | bytes 262144 | tf_op jit(solution)/shard_map/all_to_all | solution.py:42
  70.2 0.1 pad_add_fusion
  70.3 0.1 broadcast_compare_fusion
  70.4 12.0 %all-to-all-done.1 = bf16[8,2,32,128]{3,2,1,0:T(8,128)(2,1)S(1)} async-done(((bf16[8,2,32,128]{3,2,1,0:T(8,128)(2,1)}), bf16[8,2,32,128]{3,2,1,0:T(8,128)(2,1)S(1)}, u32[]{:S(2)}, u32[]{:S(2)}) %all-to-all-start.1) | async-done | bytes 131104 | tf_op jit(solution)/shard_map/all_to_all | solution.py:42
  82.5 0.2 fusion.6
  82.7 0.1 fusion.45
  82.8 0.2 fusion.33
  83.1 0.2 fusion.19
  83.3 0.3 multiply_reduce_fusion.1
  83.6 0.2 fusion.43
  83.9 0.7 maximum_bitcast_fusion
  84.6 4.3 %all-to-all-start.2 = ((bf16[8,2,40,128]{3,2,1,0:T(8,128)(2,1)}), bf16[8,2,40,128]{3,2,1,0:T(8,128)(2,1)S(1)}, u32[]{:S(2)}, u32[]{:S(2)}) async-start(bf16[8,2,40,128]{3,2,1,0:T(8,128)(2,1)} %maximum_bitcast_fusion), calls=%async_computation.2 | async-start | bytes 327680 | tf_op jit(solution)/shard_map/all_to_all | solution.py:42
  88.9 2.2 %fusion.23 = f32[2,64,4096]{2,1,0:T(8,128)} fusion(bf16[2,128,128]{2,1,0:T(8,128)(2,1)S(1)} %get-tuple-element.41, bf16[1,2,4096,128]{3,2,1,0:T(8,128)(2,1)S(1)} %copy-done), kind=kOutput, calls=%fused_computation.56 | convolution fusion | flops 134217728 | bytes 4227072 | tf_op jit(solution)/shard_map/nth,ndh->ntd/dot_general | solution.py:199
  91.1 10.5 %all-to-all-done.2 = bf16[8,2,40,128]{3,2,1,0:T(8,128)(2,1)S(1)} async-done(((bf16[8,2,40,128]{3,2,1,0:T(8,128)(2,1)}), bf16[8,2,40,128]{3,2,1,0:T(8,128)(2,1)S(1)}, u32[]{:S(2)}, u32[]{:S(2)}) %all-to-all-start.2) | async-done | bytes 163872 | tf_op jit(solution)/shard_map/all_to_all | solution.py:42
  101.6 3.1 %fusion.2 = bf16[2,64,4096]{2,1,0:T(8,128)(2,1)} fusion(f32[2,64,4096]{2,1,0:T(8,128)} %fusion.23, bf16[2,40,128]{2,1,0:T(8,128)(2,1)S(1)} %convert.30, bf16[2,16,4096]{2,1,0:T(8,128)(2,1)S(1)} %bitcast.78, bf16[2,16,4096]{2,1,0:T(8,128)(2,1)S(1)} %bitcast.81), kind=kOutput, calls=%fused_computation.4 | convolution fusion | flops 35651584 | bytes 3686400 | tf_op jit(solution)/shard_map/nct,ncd->ntd/dot_general | solution.py:201
  104.8 1.9 %collective-permute-start.6 = (bf16[2,64,4096]{2,1,0:T(8,128)(2,1)}, bf16[2,64,4096]{2,1,0:T(8,128)(2,1)}, u32[]{:S(2)}, u32[]{:S(2)}) collective-permute-start(bf16[2,64,4096]{2,1,0:T(8,128)(2,1)} %fusion.2), channel_id=1, source_target_pairs={{0,8},{8,0},{16,24},{24,16},{32,40},{40,32},{48,56},{56,48},{64,72... | collective-permute-start | bytes 3145736 | tf_op jit(solution)/shard_map/ppermute | solution.py:20
  106.7 0.8 fusion.25
  107.5 2.1 %collective-permute-done.6 = bf16[2,64,4096]{2,1,0:T(8,128)(2,1)} collective-permute-done((bf16[2,64,4096]{2,1,0:T(8,128)(2,1)}, bf16[2,64,4096]{2,1,0:T(8,128)(2,1)}, u32[]{:S(2)}, u32[]{:S(2)}) %collective-permute-start.6) | collective-permute-done | bytes 1048608 | tf_op jit(solution)/shard_map/ppermute | solution.py:20
  109.6 1.7 convert_add_fusion
  111.4 0.1 dynamic-slice_convert_fusion
  111.5 2.6 %collective-permute-start.7 = (bf16[2,32,2048]{2,1,0:T(8,128)(2,1)S(1)}, bf16[2,32,2048]{2,1,0:T(8,128)(2,1)S(1)}, u32[]{:S(2)}, u32[]{:S(2)}) collective-permute-start(bf16[2,32,2048]{2,1,0:T(8,128)(2,1)S(1)} %get-tuple-element.18), channel_id=1, source_target_pairs={{0,16},{8,24},{16,0},{24,8},{32,48},{40,56},{48,32},{56,40},{64,80... | collective-permute-start | bytes 786440 | tf_op jit(solution)/shard_map/ppermute | solution.py:20
  114.1 7.6 %collective-permute-done.7 = bf16[2,32,2048]{2,1,0:T(8,128)(2,1)S(1)} collective-permute-done((bf16[2,32,2048]{2,1,0:T(8,128)(2,1)S(1)}, bf16[2,32,2048]{2,1,0:T(8,128)(2,1)S(1)}, u32[]{:S(2)}, u32[]{:S(2)}) %collective-permute-start.7) | collective-permute-done | bytes 262176 | tf_op jit(solution)/shard_map/ppermute | solution.py:20
  121.8 0.7 pad_maximum_fusion.2
  122.5 3.5 %all-to-all-start.3 = ((bf16[4,2,32,512]{3,2,1,0:T(8,128)(2,1)}), bf16[4,2,32,512]{3,2,1,0:T(8,128)(2,1)S(1)}, u32[]{:S(2)}, u32[]{:S(2)}) async-start(bf16[4,2,32,512]{3,2,1,0:T(8,128)(2,1)} %pad_maximum_fusion.2), calls=%async_computation.3 | async-start | bytes 524288 | tf_op jit(solution)/shard_map/all_to_all | solution.py:38
  126.1 2.6 %collective-permute-start.8 = (bf16[2,32,2048]{2,1,0:T(8,128)(2,1)S(1)}, bf16[2,32,2048]{2,1,0:T(8,128)(2,1)S(1)}, u32[]{:S(2)}, u32[]{:S(2)}) collective-permute-start(bf16[2,32,2048]{2,1,0:T(8,128)(2,1)S(1)} %get-tuple-element.17), channel_id=1, source_target_pairs={{0,16},{8,24},{16,0},{24,8},{32,48},{40,56},{48,32},{56,40},{64,80... | collective-permute-start | bytes 786440 | tf_op jit(solution)/shard_map/ppermute | solution.py:20
  128.7 0.1 constant_dynamic-slice_fusion
  128.8 5.8 %all-to-all-done.3 = bf16[4,2,32,512]{3,2,1,0:T(8,128)(2,1)S(1)} async-done(((bf16[4,2,32,512]{3,2,1,0:T(8,128)(2,1)}), bf16[4,2,32,512]{3,2,1,0:T(8,128)(2,1)S(1)}, u32[]{:S(2)}, u32[]{:S(2)}) %all-to-all-start.3) | async-done | bytes 262176 | tf_op jit(solution)/shard_map/all_to_all | solution.py:38
  134.7 0.8 collective-permute-done.8
  135.5 0.7 pad_maximum_fusion.3
  136.3 4.8 %all-to-all-start.4 = ((bf16[4,2,32,512]{3,2,1,0:T(8,128)(2,1)}), bf16[4,2,32,512]{3,2,1,0:T(8,128)(2,1)S(1)}, u32[]{:S(2)}, u32[]{:S(2)}) async-start(bf16[4,2,32,512]{3,2,1,0:T(8,128)(2,1)} %pad_maximum_fusion.3), calls=%async_computation.4 | async-start | bytes 524288 | tf_op jit(solution)/shard_map/all_to_all | solution.py:38
  141.0 0.1 slice.121
  141.1 1.9 %collective-permute-start.10 = (f32[2,64]{1,0:T(2,128)S(1)}, f32[2,64]{1,0:T(2,128)S(1)}, u32[]{:S(2)}, u32[]{:S(2)}) collective-permute-start(f32[2,64]{1,0:T(2,128)S(1)} %slice.121), channel_id=1, source_target_pairs={{0,8},{8,0},{16,24},{24,16},{32,40},{40,32},{48,56},{56,48},{64,72... | collective-permute-start | bytes 1544 | tf_op jit(solution)/shard_map/ppermute | solution.py:20
  143.0 1.1 collective-permute-done.10
  144.2 0.1 slice.123
  144.2 2.6 %collective-permute-start.11 = (f32[2,32]{1,0:T(2,128)S(1)}, f32[2,32]{1,0:T(2,128)S(1)}, u32[]{:S(2)}, u32[]{:S(2)}) collective-permute-start(f32[2,32]{1,0:T(2,128)S(1)} %slice.123), channel_id=1, source_target_pairs={{0,16},{8,24},{16,0},{24,8},{32,48},{40,56},{48,32},{56,40},{64,80... | collective-permute-start | bytes 776 | tf_op jit(solution)/shard_map/ppermute | solution.py:20
  146.9 0.9 slice_reduce_fusion
  147.7 2.0 %collective-permute-done.11 = f32[2,32]{1,0:T(2,128)S(1)} collective-permute-done((f32[2,32]{1,0:T(2,128)S(1)}, f32[2,32]{1,0:T(2,128)S(1)}, u32[]{:S(2)}, u32[]{:S(2)}) %collective-permute-start.11) | collective-permute-done | bytes 288 | tf_op jit(solution)/shard_map/ppermute | solution.py:20
  149.7 3.5 %collective-permute-start.9 = (bf16[2,32,512]{2,1,0:T(8,128)(2,1)S(1)}, bf16[2,32,512]{2,1,0:T(8,128)(2,1)S(1)}, u32[]{:S(2)}, u32[]{:S(2)}) collective-permute-start(bf16[2,32,512]{2,1,0:T(8,128)(2,1)S(1)} %reduce_sum.71), channel_id=1, source_target_pairs={{0,4},{1,5},{2,6},{3,7},{4,0},{5,1},{6,2},{7,3},{8,12},{9,13},{10,... | collective-permute-start | bytes 196616 | tf_op jit(solution)/shard_map/ppermute | solution.py:20
  153.3 10.2 %collective-permute-done.9 = bf16[2,32,512]{2,1,0:T(8,128)(2,1)S(1)} collective-permute-done((bf16[2,32,512]{2,1,0:T(8,128)(2,1)S(1)}, bf16[2,32,512]{2,1,0:T(8,128)(2,1)S(1)}, u32[]{:S(2)}, u32[]{:S(2)}) %collective-permute-start.9) | collective-permute-done | bytes 65568 | tf_op jit(solution)/shard_map/ppermute | solution.py:20
  163.5 0.1 fusion.17
  163.6 18.8 %collective-permute-start.12 = (bf16[2,32,512]{2,1,0:T(8,128)(2,1)S(1)}, bf16[2,32,512]{2,1,0:T(8,128)(2,1)S(1)}, u32[]{:S(2)}, u32[]{:S(2)}) collective-permute-start(bf16[2,32,512]{2,1,0:T(8,128)(2,1)S(1)} %fusion.17), channel_id=1, source_target_pairs={{0,992},{8,1000},{16,1008},{24,1016},{32,0},{40,8},{48,16},{56,24}... | collective-permute-start | bytes 196616 | tf_op jit(solution)/shard_map/ppermute | solution.py:25
  182.4 1.9 %collective-permute-done.12 = bf16[2,32,512]{2,1,0:T(8,128)(2,1)S(1)} collective-permute-done((bf16[2,32,512]{2,1,0:T(8,128)(2,1)S(1)}, bf16[2,32,512]{2,1,0:T(8,128)(2,1)S(1)}, u32[]{:S(2)}, u32[]{:S(2)}) %collective-permute-start.12) | collective-permute-done | bytes 65568 | tf_op jit(solution)/shard_map/ppermute | solution.py:25
  184.3 0.6 fusion.18
  (56 shorter events, 0.6 us)
Async XLA Ops:
  0.0 23.4 %copy-start.8 = (bf16[1,2,2,1024]{3,2,1,0:T(2,128)(2,1)S(1)}, bf16[1,2,2,1024]{3,2,1,0:T(2,128)(2,1)}, u32[]{:S(2)}) copy-start(bf16[1,2,2,1024]{3,2,1,0:T(2,128)(2,1)} %param.12) | copy-start | bytes 24580
  0.0 23.4 %copy-start.9 = (s32[1,2,32]{2,1,0:T(2,128)S(1)}, s32[1,2,32]{2,1,0:T(2,128)}, u32[]{:S(2)}) copy-start(s32[1,2,32]{2,1,0:T(2,128)} %param.11) | copy-start | bytes 772
  0.0 30.8 %copy-start.2 = (bf16[1,2,4096,16]{2,3,1,0:T(8,128)(2,1)S(1)}, bf16[1,2,4096,16]{2,3,1,0:T(8,128)(2,1)}, u32[]{:S(2)}) copy-start(bf16[1,2,4096,16]{2,3,1,0:T(8,128)(2,1)} %param.15) | copy-start | bytes 786436
  0.0 13.5 %collective-permute-start = (bf16[2,32,512]{2,1,0:T(8,128)(2,1)}, bf16[2,32,512]{2,1,0:T(8,128)(2,1)S(1)}, u32[]{:S(2)}, u32[]{:S(2)}) collective-permute-start(bf16[2,32,512]{2,1,0:T(8,128)(2,1)} %bitcast.84), channel_id=1, source_target_pairs={{0,4},{1,5},{2,6},{3,7},{4,0},{5,1},{6,2},{7,3},{8,12},{9,13},{10,... | collective-permute-start | bytes 196616 | tf_op jit(solution)/shard_map/ppermute | solution.py:20
  14.4 42.6 %copy-start = (bf16[1,2,4096,128]{3,2,1,0:T(8,128)(2,1)S(1)}, bf16[1,2,4096,128]{3,2,1,0:T(8,128)(2,1)}, u32[]{:S(2)}) copy-start(bf16[1,2,4096,128]{3,2,1,0:T(8,128)(2,1)} %param.13) | copy-start | bytes 6291460
  15.2 22.7 %all-to-all-start = ((bf16[4,2,2,32,512]{4,3,2,1,0:T(8,128)(2,1)}), bf16[4,2,2,32,512]{4,3,2,1,0:T(8,128)(2,1)S(1)}, u32[]{:S(2)}, u32[]{:S(2)}) async-start(bf16[4,2,2,32,512]{4,3,2,1,0:T(8,128)(2,1)} %pad_maximum_fusion), calls=%async_computation | async-start | bytes 1048576 | tf_op jit(solution)/shard_map/all_to_all | solution.py:38
  23.5 17.5 %collective-permute-start.4 = (bf16[2,2176]{1,0:T(2,128)(2,1)S(1)}, bf16[2,2176]{1,0:T(2,128)(2,1)S(1)}, u32[]{:S(2)}, u32[]{:S(2)}) collective-permute-start(bf16[2,2176]{1,0:T(2,128)(2,1)S(1)} %fusion.34), channel_id=1, source_target_pairs={{0,16},{8,24},{16,0},{24,8},{32,48},{40,56},{48,32},{56,40},{64,80... | collective-permute-start | bytes 26120 | tf_op jit(solution)/shard_map/ppermute | solution.py:20
  37.9 14.9 %collective-permute-start.1 = (bf16[4,2,2,32,512]{4,3,2,1,0:T(8,128)(2,1)S(1)}, bf16[4,2,2,32,512]{4,3,2,1,0:T(8,128)(2,1)}, u32[]{:S(2)}, u32[]{:S(2)}) collective-permute-start(bf16[4,2,2,32,512]{4,3,2,1,0:T(8,128)(2,1)S(1)} %all-to-all-done.refs_0_), channel_id=1, source_target_pairs={{0,16},{8,24},{16,0},{24,8},{32,48},{40,56},{48,32},{56,40},{64,80... | collective-permute-start | bytes 1572872 | tf_op jit(solution)/shard_map/ppermute | solution.py:20
  41.0 3.1 %collective-permute-start.5 = (bf16[2,2,2176]{2,1,0:T(2,128)(2,1)S(1)}, bf16[2,2,2176]{2,1,0:T(2,128)(2,1)S(1)}, u32[]{:S(2)}, u32[]{:S(2)}) collective-permute-start(bf16[2,2,2176]{2,1,0:T(2,128)(2,1)S(1)} %pad_maximum_fusion.7), channel_id=1, source_target_pairs={{0,8},{8,0},{16,24},{24,16},{32,40},{40,32},{48,56},{56,48},{64,72... | collective-permute-start | bytes 52232 | tf_op jit(solution)/shard_map/ppermute | solution.py:20
  44.1 11.1 %collective-permute-start.2 = (bf16[4,2,2,32,512]{4,3,2,1,0:T(8,128)(2,1)S(1)}, bf16[4,2,2,32,512]{4,3,2,1,0:T(8,128)(2,1)}, u32[]{:S(2)}, u32[]{:S(2)}) collective-permute-start(bf16[4,2,2,32,512]{4,3,2,1,0:T(8,128)(2,1)S(1)} %all-to-all-done.refs_0_), channel_id=1, source_target_pairs={{0,8},{8,0},{16,24},{24,16},{32,40},{40,32},{48,56},{56,48},{64,72... | collective-permute-start | bytes 1572872 | tf_op jit(solution)/shard_map/ppermute | solution.py:20
  52.9 4.1 %collective-permute-start.3 = (bf16[4,2,2,32,512]{4,3,2,1,0:T(8,128)(2,1)}, bf16[4,2,2,32,512]{4,3,2,1,0:T(8,128)(2,1)}, u32[]{:S(2)}, u32[]{:S(2)}) collective-permute-start(bf16[4,2,2,32,512]{4,3,2,1,0:T(8,128)(2,1)} %collective-permute-done.1.refs_1_), channel_id=1, source_target_pairs={{0,8},{8,0},{16,24},{24,16},{32,40},{40,32},{48,56},{56,48},{64,72... | collective-permute-start | bytes 1572872 | tf_op jit(solution)/shard_map/ppermute | solution.py:20
  57.0 13.3 %copy-start.7 = (bf16[1,2,128,128]{3,2,1,0:T(8,128)(2,1)S(1)}, bf16[1,2,128,128]{3,2,1,0:T(8,128)(2,1)}, u32[]{:S(2)}) copy-start(bf16[1,2,128,128]{3,2,1,0:T(8,128)(2,1)} %param.10) | copy-start | bytes 196612
  60.5 0.6 copy-start.1
  61.8 20.6 %all-to-all-start.1 = ((bf16[8,2,32,128]{3,2,1,0:T(8,128)(2,1)}), bf16[8,2,32,128]{3,2,1,0:T(8,128)(2,1)S(1)}, u32[]{:S(2)}, u32[]{:S(2)}) async-start(bf16[8,2,32,128]{3,2,1,0:T(8,128)(2,1)} %broadcast_in_dim.79), calls=%async_computation.1 | async-start | bytes 262144 | tf_op jit(solution)/shard_map/all_to_all | solution.py:42
  84.6 17.0 %all-to-all-start.2 = ((bf16[8,2,40,128]{3,2,1,0:T(8,128)(2,1)}), bf16[8,2,40,128]{3,2,1,0:T(8,128)(2,1)S(1)}, u32[]{:S(2)}, u32[]{:S(2)}) async-start(bf16[8,2,40,128]{3,2,1,0:T(8,128)(2,1)} %maximum_bitcast_fusion), calls=%async_computation.2 | async-start | bytes 327680 | tf_op jit(solution)/shard_map/all_to_all | solution.py:42
  88.9 12.7 %copy-start.3 = (bf16[1,2,4096,16]{2,3,1,0:T(8,128)(2,1)S(1)}, bf16[1,2,4096,16]{2,3,1,0:T(8,128)(2,1)}, u32[]{:S(2)}) copy-start(bf16[1,2,4096,16]{2,3,1,0:T(8,128)(2,1)} %param.15) | copy-start | bytes 786436
  88.9 12.7 %copy-start.4 = (bf16[1,2,4096,16]{2,3,1,0:T(8,128)(2,1)S(1)}, bf16[1,2,4096,16]{2,3,1,0:T(8,128)(2,1)}, u32[]{:S(2)}) copy-start(bf16[1,2,4096,16]{2,3,1,0:T(8,128)(2,1)} %param.14) | copy-start | bytes 786436
  104.8 4.9 %collective-permute-start.6 = (bf16[2,64,4096]{2,1,0:T(8,128)(2,1)}, bf16[2,64,4096]{2,1,0:T(8,128)(2,1)}, u32[]{:S(2)}, u32[]{:S(2)}) collective-permute-start(bf16[2,64,4096]{2,1,0:T(8,128)(2,1)} %fusion.2), channel_id=1, source_target_pairs={{0,8},{8,0},{16,24},{24,16},{32,40},{40,32},{48,56},{56,48},{64,72... | collective-permute-start | bytes 3145736 | tf_op jit(solution)/shard_map/ppermute | solution.py:20
  111.5 10.2 %collective-permute-start.7 = (bf16[2,32,2048]{2,1,0:T(8,128)(2,1)S(1)}, bf16[2,32,2048]{2,1,0:T(8,128)(2,1)S(1)}, u32[]{:S(2)}, u32[]{:S(2)}) collective-permute-start(bf16[2,32,2048]{2,1,0:T(8,128)(2,1)S(1)} %get-tuple-element.18), channel_id=1, source_target_pairs={{0,16},{8,24},{16,0},{24,8},{32,48},{40,56},{48,32},{56,40},{64,80... | collective-permute-start | bytes 786440 | tf_op jit(solution)/shard_map/ppermute | solution.py:20
  122.5 41.0 %copy-start.5 = (bf16[1,2,32,512]{3,2,1,0:T(8,128)(2,1)S(1)}, bf16[1,2,32,512]{3,2,1,0:T(8,128)(2,1)}, u32[]{:S(2)}) copy-start(bf16[1,2,32,512]{3,2,1,0:T(8,128)(2,1)} %param.8) | copy-start | bytes 196612
  122.5 41.0 %copy-start.6 = (bf16[1,2,32,512]{3,2,1,0:T(8,128)(2,1)S(1)}, bf16[1,2,32,512]{3,2,1,0:T(8,128)(2,1)}, u32[]{:S(2)}) copy-start(bf16[1,2,32,512]{3,2,1,0:T(8,128)(2,1)} %param.9) | copy-start | bytes 196612
  122.5 12.1 %all-to-all-start.3 = ((bf16[4,2,32,512]{3,2,1,0:T(8,128)(2,1)}), bf16[4,2,32,512]{3,2,1,0:T(8,128)(2,1)S(1)}, u32[]{:S(2)}, u32[]{:S(2)}) async-start(bf16[4,2,32,512]{3,2,1,0:T(8,128)(2,1)} %pad_maximum_fusion.2), calls=%async_computation.3 | async-start | bytes 524288 | tf_op jit(solution)/shard_map/all_to_all | solution.py:38
  126.1 9.4 %collective-permute-start.8 = (bf16[2,32,2048]{2,1,0:T(8,128)(2,1)S(1)}, bf16[2,32,2048]{2,1,0:T(8,128)(2,1)S(1)}, u32[]{:S(2)}, u32[]{:S(2)}) collective-permute-start(bf16[2,32,2048]{2,1,0:T(8,128)(2,1)S(1)} %get-tuple-element.17), channel_id=1, source_target_pairs={{0,16},{8,24},{16,0},{24,8},{32,48},{40,56},{48,32},{56,40},{64,80... | collective-permute-start | bytes 786440 | tf_op jit(solution)/shard_map/ppermute | solution.py:20
  136.3 16.9 %all-to-all-start.4 = ((bf16[4,2,32,512]{3,2,1,0:T(8,128)(2,1)}), bf16[4,2,32,512]{3,2,1,0:T(8,128)(2,1)S(1)}, u32[]{:S(2)}, u32[]{:S(2)}) async-start(bf16[4,2,32,512]{3,2,1,0:T(8,128)(2,1)} %pad_maximum_fusion.3), calls=%async_computation.4 | async-start | bytes 524288 | tf_op jit(solution)/shard_map/all_to_all | solution.py:38
  141.1 3.0 %collective-permute-start.10 = (f32[2,64]{1,0:T(2,128)S(1)}, f32[2,64]{1,0:T(2,128)S(1)}, u32[]{:S(2)}, u32[]{:S(2)}) collective-permute-start(f32[2,64]{1,0:T(2,128)S(1)} %slice.121), channel_id=1, source_target_pairs={{0,8},{8,0},{16,24},{24,16},{32,40},{40,32},{48,56},{56,48},{64,72... | collective-permute-start | bytes 1544 | tf_op jit(solution)/shard_map/ppermute | solution.py:20
  144.2 5.5 %collective-permute-start.11 = (f32[2,32]{1,0:T(2,128)S(1)}, f32[2,32]{1,0:T(2,128)S(1)}, u32[]{:S(2)}, u32[]{:S(2)}) collective-permute-start(f32[2,32]{1,0:T(2,128)S(1)} %slice.123), channel_id=1, source_target_pairs={{0,16},{8,24},{16,0},{24,8},{32,48},{40,56},{48,32},{56,40},{64,80... | collective-permute-start | bytes 776 | tf_op jit(solution)/shard_map/ppermute | solution.py:20
  149.7 13.8 %collective-permute-start.9 = (bf16[2,32,512]{2,1,0:T(8,128)(2,1)S(1)}, bf16[2,32,512]{2,1,0:T(8,128)(2,1)S(1)}, u32[]{:S(2)}, u32[]{:S(2)}) collective-permute-start(bf16[2,32,512]{2,1,0:T(8,128)(2,1)S(1)} %reduce_sum.71), channel_id=1, source_target_pairs={{0,4},{1,5},{2,6},{3,7},{4,0},{5,1},{6,2},{7,3},{8,12},{9,13},{10,... | collective-permute-start | bytes 196616 | tf_op jit(solution)/shard_map/ppermute | solution.py:20
  163.6 20.7 %collective-permute-start.12 = (bf16[2,32,512]{2,1,0:T(8,128)(2,1)S(1)}, bf16[2,32,512]{2,1,0:T(8,128)(2,1)S(1)}, u32[]{:S(2)}, u32[]{:S(2)}) collective-permute-start(bf16[2,32,512]{2,1,0:T(8,128)(2,1)S(1)} %fusion.17), channel_id=1, source_target_pairs={{0,992},{8,1000},{16,1008},{24,1016},{32,0},{40,8},{48,16},{56,24}... | collective-permute-start | bytes 196616 | tf_op jit(solution)/shard_map/ppermute | solution.py:25
